TPU v7x, 768 devices: a whole 4x8x12 slice. The times are simulated.
768 devices in a mesh: dp: 64 (over z_hi, y, x), mp: 12 (over z_lo, core).
Axes of the slice: x: 4, y: 8, z: 12 (z_hi: 2, z_lo: 6; z = z_hi * 6 + z_lo), core: 2. Of those that a mesh axis runs over, the one named last changes fastest.
Arguments:
- tokens: bfloat16 [32768, 3072], P('dp', 'mp'), may hold values from -150 to 150
- pre_gain: bfloat16 [3072], P('mp'), may hold values from 0.25 to 1.75
- input_weight: bfloat16 [3, 3072, 3072], P(None, 'dp', 'mp'), may hold values from -0.078125 to 0.078125
- output_weight: bfloat16 [3072, 3072], P('mp', 'dp'), may hold values from -1.25 to 1.25
- position_bias: bfloat16 [48, 512, 512], P('mp'), may hold values from -3 to 353
- post_gain: bfloat16 [3072], P('mp'), may hold values from 0.25 to 1.75
Outputs:
- stream: bfloat16 [32768, 3072], P('dp', 'mp')
- normed: bfloat16 [32768, 3072], P('dp', 'mp')
All inputs are finite; a program needn't handle non-finite values.
Results may differ from a plain program's by a relative error of at most 0.013.
Values may be sent and summed in bfloat16 or wider, within the bound.
A program may use at most 64 MiB of HBM per device.

v0:
```python
import jax
import jax.numpy as jnp
from jax import lax
from jax.sharding import PartitionSpec as P

epsilon = 1e-06


def gather_turned(arrays, axis, dims):
    turned = [jnp.moveaxis(a, dim, 0) for a, dim in zip(arrays, dims)]
    both = jnp.concatenate([t.reshape(len(t), -1) for t in turned], axis=1)
    whole, at, gathered = (lax.all_gather(both, axis, axis=0, tiled=True), 0, [])
    for t, dim in zip(turned, dims):
        slab = whole[:, at : at + t[0].size].reshape(-1, *t.shape[1:])
        gathered.append(jnp.moveaxis(slab, 0, dim))
        at += t[0].size
    return tuple(gathered)


def copy_for_each(array, axis):
    size = lax.axis_size(axis)
    return lax.all_to_all(
        jnp.broadcast_to(array[None], (size, *array.shape)), axis, 0, 0, tiled=True
    )


def of_everyone(array, axis):
    everything = copy_for_each(array, axis)
    return jnp.sum(everything, axis=0)


def attend_all(mixed_heads, position_bias):
    row_count = mixed_heads.shape[1]
    inner_width = mixed_heads.shape[2]
    head_count = position_bias.shape[0]
    seq_len = position_bias.shape[1]
    grouped = mixed_heads.reshape(
        3, row_count // seq_len, seq_len, head_count, inner_width // head_count
    )
    bias_wide = position_bias.astype(jnp.float32)

    def one_sequence(sequence):
        sequence_block = lax.dynamic_index_in_dim(grouped, sequence, 1, keepdims=False)
        scores = (
            jnp.einsum(
                "qhd,khd->hqk",
                sequence_block[0],
                sequence_block[1],
                preferred_element_type=jnp.float32,
            )
            + bias_wide
        )
        row_max = jnp.max(scores, axis=2, keepdims=True)
        weights = jnp.exp(scores - row_max)
        probabilities = (weights / jnp.sum(weights, axis=2, keepdims=True)).astype(jnp.bfloat16)
        context = jnp.einsum(
            "hqk,khd->qhd", probabilities, sequence_block[2], preferred_element_type=jnp.float32
        )
        return context.reshape(seq_len, inner_width).astype(jnp.bfloat16)

    stacked = lax.map(one_sequence, jnp.arange(row_count // seq_len, dtype=jnp.int32))
    return stacked.reshape(row_count, inner_width)


def on_device(tokens, pre_gain, input_weight, output_weight, position_bias, post_gain):
    rows_all, gain_all = (
        lax.all_gather(tokens, "mp", axis=1, tiled=True),
        lax.all_gather(pre_gain, "mp", axis=0, tiled=True),
    )
    widened = rows_all.astype(jnp.float32)
    inverse_rms = lax.rsqrt(jnp.mean(widened * widened, axis=1, keepdims=True) + epsilon)
    normed_in = (widened * inverse_rms * gain_all.astype(jnp.float32)).astype(jnp.bfloat16)
    feature_count = tokens.shape[1]
    input_full, output_full = gather_turned((input_weight, output_weight), "dp", (1, 1))
    projected = jnp.einsum("td,kdi->kti", normed_in, input_full, preferred_element_type=jnp.float32)
    context = attend_all(projected.astype(jnp.bfloat16), position_bias)
    partial_value = jnp.dot(context, output_full, preferred_element_type=jnp.float32)
    attention_out = lax.psum_scatter(
        partial_value.astype(jnp.bfloat16), "mp", scatter_dimension=1, tiled=True
    ).astype(jnp.float32)
    stream = (tokens.astype(jnp.float32) + attention_out).astype(jnp.bfloat16)
    restored = lax.optimization_barrier(stream).astype(jnp.float32)
    squares = of_everyone(jnp.sum(restored * restored, axis=1), "mp")
    post_rms = lax.rsqrt(squares[:, None] / (feature_count * lax.axis_size("mp")) + epsilon)
    normed = (restored * post_rms * post_gain.astype(jnp.float32)).astype(jnp.bfloat16)
    return (stream, normed)


def solution(mesh):
    return jax.shard_map(
        on_device,
        mesh=mesh,
        in_specs=(
            P("dp", "mp"),
            P("mp"),
            P(None, "dp", "mp"),
            P("mp", "dp"),
            P("mp", None, None),
            P("mp"),
        ),
        out_specs=(P("dp", "mp"), P("dp", "mp")),
        check_vma=False,
    )
```

profile of v0, /device:TPU:1, one launch (start us, length us, event | category | flops | bytes accessed | tf_op | source)
XLA Modules:
  0.0 429.9 jit_solution(16377624813672957801)
XLA Ops:
  7.2 0.7 all-gather.6.cloned.1.call-update
  7.9 0.9 copy.24
  8.8 1.4 pad_maximum_fusion
  10.2 0.0 reduce-scatter.2.cloned.1.call-start
  10.3 0.7 reshape.52
  11.0 30.1 %all-gather = bf16[12,1,256]{2,1,0:T(2,128)(2,1)S(1)} all-gather(bf16[1,1,256]{2,1,0:T(2,128)(2,1)S(1)} %reshape.52), channel_id=1, replica_groups=mesh['dp'=64,'mp'=12] {'mp'}, dimensions={0}, use_global_device_ids=true | all-gather | bytes 6656 | tf_op jit(solution)/shard_map/all_gather | solution.py:68
  41.1 4.2 copy.21
  45.2 40.7 %all-gather.6.cloned.1.call-done = bf16[512,3072]{1,0:T(8,128)(2,1)} async-done(((bf16[512,256]{1,0:T(8,128)(2,1)}), bf16[512,3072]{1,0:T(8,128)(2,1)}) %all-gather.6.cloned.1.call-update) | async-done | bytes 3145744 | tf_op jit(solution)/shard_map/all_gather | solution.py:67
  85.9 2.6 fusion.1
  88.5 216.8 %all-gather.4.cloned.1.call-done = bf16[3072,1024]{1,0:T(8,128)(2,1)} async-done(((bf16[48,1024]{1,0:T(8,128)(2,1)}), bf16[3072,1024]{1,0:T(8,128)(2,1)}) %all-gather.4.cloned.1.call-update) | async-done | bytes 6291472 | tf_op jit(solution)/shard_map/all_gather | solution.py:12
  305.4 4.8 %slice.26 = bf16[3072,768]{1,0:T(8,128)(2,1)} slice(bf16[3072,1024]{1,0:T(8,128)(2,1)} %all-gather.4.cloned.1.call-done), slice={[0:3072], [0:768]} | slice | bytes 9437184 | tf_op jit(solution)/shard_map/slice | solution.py:14
  310.2 6.9 %copy.20 = bf16[3072,768]{0,1:T(8,128)(2,1)} copy(bf16[3072,768]{1,0:T(8,128)(2,1)} %slice.26) | data formatting | bytes 9437184 | tf_op jit(solution)/shard_map/slice | solution.py:14
  317.1 5.0 %fusion.15 = bf16[3,512,256]{1,2,0:T(8,128)(2,1)S(1)} fusion(bf16[3,3072,256]{1,2,0:T(8,128)(2,1)} %bitcast.30, bf16[512,3072]{1,0:T(8,128)(2,1)S(1)} %copy-done, f32[3072]{0:T(1024)S(1)} %bitcast.40, f32[512]{0:T(512)S(1)} %add_rsqrt_fusion.1), kind=kOutput, calls=%fused_computation.18 | convolution fusion | flops 2422603776 | bytes 8665088 | tf_op jit(solution)/shard_map/td,kdi->kti/dot_general | solution.py:75
  322.1 0.1 fusion.25
  322.2 3.0 fusion.26
  325.2 3.5 fusion.18
  328.7 4.2 convolution_convert_fusion
  332.9 70.3 %reduce-scatter.2.cloned.1.call-done = bf16[512,256]{1,0:T(8,128)(2,1)} async-done(((bf16[512,3072]{1,0:T(8,128)(2,1)}), bf16[512,256]{1,0:T(8,128)(2,1)}) %reduce-scatter.2.cloned.1.call-update) | async-done | bytes 262160 | tf_op jit(solution)/shard_map/reduce_scatter | solution.py:78
  403.3 1.0 add_convert_fusion
  404.3 0.1 fusion.19
  404.4 0.6 broadcast_in_dim.9
  405.1 9.0 %all-to-all-start = ((f32[12,1,512]{2,1,0:T(1,128)}), f32[12,1,512]{2,1,0:T(1,128)S(1)}, u32[]{:S(2)}, u32[]{:S(2)}) async-start(f32[12,1,512]{2,1,0:T(1,128)} %broadcast_in_dim.9), calls=%async_computation.1 | async-start | bytes 49152 | tf_op jit(solution)/shard_map/all_to_all | solution.py:22
  414.1 8.4 %all-to-all-done = f32[12,1,512]{2,1,0:T(1,128)S(1)} async-done(((f32[12,1,512]{2,1,0:T(1,128)}), f32[12,1,512]{2,1,0:T(1,128)S(1)}, u32[]{:S(2)}, u32[]{:S(2)}) %all-to-all-start) | async-done | bytes 24608 | tf_op jit(solution)/shard_map/all_to_all | solution.py:22
  422.5 0.8 fusion.21
  (17 shorter events, 0.2 us)
Async XLA Ops:
  7.2 78.8 %all-gather.6.cloned.1.call-start = ((), (), s32[]{:S(2)}) async-start(), calls=%async_computation.3 | async-start | bytes 3407872 | tf_op jit(solution)/shard_map/all_gather | solution.py:67
  7.9 297.5 %all-gather.4.cloned.1.call-start = ((), (), s32[]{:S(2)}) async-start(), calls=%async_computation.2 | async-start | bytes 6389760 | tf_op jit(solution)/shard_map/all_gather | solution.py:12
  10.2 393.0 %reduce-scatter.2.cloned.1.call-start = ((), (), s32[]{:S(2)}) async-start(), calls=%async_computation.4 | async-start | bytes 3407872 | tf_op jit(solution)/shard_map/reduce_scatter | solution.py:78
  310.2 6.9 %copy-start = (bf16[512,3072]{1,0:T(8,128)(2,1)S(1)}, bf16[512,3072]{1,0:T(8,128)(2,1)}, u32[]{:S(2)}) copy-start(bf16[512,3072]{1,0:T(8,128)(2,1)} %all-gather.6.cloned.1.call-done) | copy-start | bytes 9437188
  328.7 74.6 %copy-start.2 = (bf16[512,256]{1,0:T(8,128)(2,1)S(1)}, bf16[512,256]{1,0:T(8,128)(2,1)}, u32[]{:S(2)}) copy-start(bf16[512,256]{1,0:T(8,128)(2,1)} %param.6) | copy-start | bytes 786436
  328.7 85.3 %copy-start.3 = (bf16[256]{0:T(256)(128)(2,1)S(1)}, bf16[256]{0:T(256)(128)(2,1)}, u32[]{:S(2)}) copy-start(bf16[256]{0:T(256)(128)(2,1)} %param.11) | copy-start | bytes 1540
  404.3 19.1 %copy-start.1 = (bf16[512,256]{1,0:T(8,128)(2,1)}, bf16[512,256]{1,0:T(8,128)(2,1)S(1)}, u32[]{:S(2)}) copy-start(bf16[512,256]{1,0:T(8,128)(2,1)S(1)} %add_convert_fusion) | copy-start | bytes 786436
  405.1 17.4 %all-to-all-start = ((f32[12,1,512]{2,1,0:T(1,128)}), f32[12,1,512]{2,1,0:T(1,128)S(1)}, u32[]{:S(2)}, u32[]{:S(2)}) async-start(f32[12,1,512]{2,1,0:T(1,128)} %broadcast_in_dim.9), calls=%async_computation.1 | async-start | bytes 49152 | tf_op jit(solution)/shard_map/all_to_all | solution.py:22
Sparse Core Ops, SparseCore 0:
  10.3 75.5 all-gather.5
  91.8 213.4 all-gather.3
  333.1 70.1 reduce-scatter.1
where the time goes:
time: 431 us; the launch traced here: 430 us
  waiting for transfers between devices  337 us (78%)
  blocking collectives  30.1 us (7%)
  local copies, waits for them, and re-layouts  18.1 us (4%)
  matrix products  15.8 us (4%)
  between operations  13.8 us (3%)
  starting transfers between devices  9.11 us (2%)
  other arithmetic  6.04 us (1%)
    all_gather x1, waiting for transfers between devices, gather_turned(): lax.all_gather(both, axis, axis=0, tiled=True)  217 us
    reduce_scatter x1, waiting for transfers between devices, on_device(): lax.psum_scatter(partial_value.astype(jnp.bfloat16), 'mp', scatter_dimens...  70.3 us
    all_gather x1, waiting for transfers between devices, on_device(): lax.all_gather(tokens, 'mp', axis=1, tiled=True)  40.7 us
    all_gather x1, blocking collectives, on_device(): lax.all_gather(pre_gain, 'mp', axis=0, tiled=True)  30.1 us
    slice x2, local copies, waits for them, and re-layouts, gather_turned(): slab = whole[:, at:at + t[0].size].reshape(-1, *t.shape[1:])  11.7 us
    all_to_all x1, starting transfers between devices, copy_for_each(): lax.all_to_all(jnp.broadcast_to(array[None], (size, *array.shape)), axis,...  8.99 us
  transfers between devices with their start and end apart: 4, of which 4 were waited for; matrix products, arithmetic and copies ran while one was open for 2% of the time, Pallas kernels for 0%

commit v1 on v0

v1 whole, which is shorter than its diff:
```python
import functools

import jax
import jax.numpy as jnp
from jax import lax
from jax.experimental import pallas as pl
from jax.experimental.pallas import tpu as pltpu
from jax.sharding import PartitionSpec as P

EPS = 1e-06
MESH = pl.DeviceIdType.MESH
F32 = jnp.float32
BF16 = jnp.bfloat16
GAIN_ROWS = 16
NH, NY, NX = 2, 8, 4
NC = 2
Q, K, V, O = 0, 1, 2, 3
XY_MATS = (Q, O)
SPLIT = 2
TCH = 2
RCH = 4


class Msg:
    def __init__(self, key, link, step, size, needs, rank):
        self.key, self.link, self.step = key, link, step
        self.size, self.needs, self.rank = size, needs, rank


def weight_messages():
    msgs = []

    def add(key, axis, step, size, needs):
        d = key[-1]
        msgs.append(Msg(key, axis + ("+" if d > 0 else "-"), step, size, needs, len(msgs)))
        return key

    def ring(name, axis, n, size, first, parity):
        got = {0: first}
        for d in (1, -1):
            needs = first
            for s in range(1, n // 2):
                needs = [add(name + (s, d), axis, s, size, needs)]
                got[-d * s] = needs
        d = 1 if parity % 2 else -1
        s = n // 2
        needs = got[-d * (s - 1)]
        got[s] = [add(name + (s, d), axis, s, size, needs)]
        return got

    for half in (0, 1):
        for m in (K, V, Q, O):
            own = [("own", m, half)]
            parity = m + half
            if m in XY_MATS:
                got = ring((m, half, "X", 0), "x", NX, 1, own, parity)
                near = got[0] + got[1] + got[-1]
                far = near + got[NX // 2]
                for g in range(SPLIT):
                    needs = near if g == 0 and SPLIT > 1 else far
                    ring((m, half, "Y", g), "y", NY, NX // SPLIT, needs, parity + g)
            else:
                got = ring((m, half, "Y", 0), "y", NY, 1, own, parity)
                order = sorted(got, key=lambda b: (abs(b), b))
                for g, b in enumerate(order):
                    ring((m, half, "X", b), "x", NX, 1, got[b], parity + g)
    return msgs


def weight_schedule(arrivals, rate=46650.0, latency=2.2, unit=24576):
    avail = dict(arrivals)
    pending = weight_messages()
    free = {"x+": 0.0, "x-": 0.0, "y+": 0.0, "y-": 0.0}
    out = []
    while pending:
        best = None
        for msg in pending:
            if all(n in avail for n in msg.needs):
                ready = max(avail[n] for n in msg.needs)
                late = 1 if msg.key[0] == O else 0
                cand = (max(ready, free[msg.link]) + 3.0 * late, msg.rank, ready)
                if best is None or cand[:2] < best[0][:2]:
                    best = (cand, msg)
        (_, _, ready), msg = best
        pending.remove(msg)
        start = max(ready, free[msg.link])
        end = start + msg.size * unit / rate
        free[msg.link] = end
        avail[msg.key] = end + latency
        out.append((start, msg))
    return out, avail


def body(
    nz, tok_in, gain_in, w_in, bias_in, pgain_in, stream_out, normed_out,
    tok, w, bias, xn, qkv, ctx, pown, sib_out, sib_in, rin, sout, sq_in,
    loc_sem, wsend, wrecv, zsend, zrecv, tsend, trecv, bsend, brecv,
    psend, precv, rsend, rrecv, qsend, qrecv,
):
    rows, cols = tok_in.shape
    blk = w_in.shape[1]
    dp, mp = lax.axis_index("dp"), lax.axis_index("mp")
    x = lax.rem(dp, NX)
    y = lax.rem(dp // NX, NY)
    zh = dp // (NX * NY)
    core = lax.rem(mp, NC)
    z = mp // NC
    n_mp = nz * NC
    heads = bias_in.shape[0]
    hd = cols // heads

    def dp_of(h, yy, xx):
        return (h * NY + yy) * NX + xx

    def wrap(v, n):
        return lax.rem(v + 2 * n, n)

    peer = {
        "x+": {"dp": dp_of(zh, y, wrap(x + 1, NX))},
        "x-": {"dp": dp_of(zh, y, wrap(x - 1, NX))},
        "y+": {"dp": dp_of(zh, wrap(y + 1, NY), x)},
        "y-": {"dp": dp_of(zh, wrap(y - 1, NY), x)},
        "zh": {"dp": dp_of(1 - zh, y, x)},
    }
    sibling = {"mp": mp + 1 - 2 * core}

    mine = pl.ds(pl.multiple_of(dp * blk, 16), blk)
    copies = [
        pltpu.make_async_copy(w_in, w.at[:, mine], loc_sem.at[0]),
        pltpu.make_async_copy(tok_in, tok.at[mp, pl.ds(0, rows)], loc_sem.at[1]),
        pltpu.make_async_copy(gain_in, tok.at[mp, pl.ds(rows, GAIN_ROWS)], loc_sem.at[2]),
        pltpu.make_async_copy(bias_in, bias, loc_sem.at[3]),
    ]
    for c in copies:
        c.start()

    barrier = pltpu.get_barrier_semaphore()
    for p in peer.values():
        pl.semaphore_signal(barrier, inc=1, device_id=p, device_id_type=MESH)
    for k in range(1, n_mp):
        other = {"mp": lax.rem(mp + k, n_mp)}
        pl.semaphore_signal(barrier, inc=1, device_id=other, device_id_type=MESH)
    pl.semaphore_wait(barrier, len(peer) + n_mp - 1)

    sends = []

    def remote(src, dst, ssem, rsem, device, keep=True):
        c = pltpu.make_async_remote_copy(
            src_ref=src, dst_ref=dst, send_sem=ssem, recv_sem=rsem,
            device_id=device, device_id_type=MESH,
        )
        c.start()
        if keep:
            sends.append(c)
        return c

    def arrival(ref, ssem, rsem):
        pltpu.make_async_remote_copy(
            src_ref=ref, dst_ref=ref, send_sem=ssem, recv_sem=rsem,
            device_id=sibling, device_id_type=MESH,
        ).wait_recv()

    def w_slot(msg, back):
        m, half, kind, g, s, d = msg.key
        h = zh if half == 0 else 1 - zh
        hop = d * (msg.step - 1 + back)
        if m in XY_MATS:
            if kind == "X":
                row, n = dp_of(h, y, wrap(x - hop, NX)), 1
            else:
                n = NX // SPLIT
                pair = lax.rem(x // n + g, SPLIT) if SPLIT > 1 else 0
                row = dp_of(h, wrap(y - hop, NY), pair * n)
        else:
            n = 1
            if kind == "Y":
                row = dp_of(h, wrap(y - hop, NY), x)
            else:
                row = dp_of(h, wrap(y + g, NY), wrap(x - hop, NX))
        return w.at[m, pl.ds(pl.multiple_of(row * blk, 16), n * blk)]

    crow = (rows + GAIN_ROWS) // TCH

    def t_slot(owner, ch):
        return tok.at[owner, pl.ds(ch * crow, crow)]

    T0 = 1.5
    arrivals = {}
    for m in (Q, K, V, O):
        arrivals["own", m, 0] = T0
    for i, m in enumerate((K, V, Q, O)):
        arrivals["own", m, 1] = T0 + 8.0 + i
    schedule, when_in = weight_schedule(arrivals)
    index = {msg.key: i for i, (_, msg) in enumerate(schedule)}
    by_key = {msg.key: msg for _, msg in schedule}
    events = [(t, 1, i, "w", msg) for i, (t, msg) in enumerate(schedule)]
    for s in range(1, nz):
        for ch in range(TCH):
            t = T0 + 2.0 + 5.8 * (s * TCH + ch + 1 - TCH) / TCH + 1.0
            events.append((t, 0, s * TCH + ch, "t", (s, ch)))
    events.sort(key=lambda e: e[:3])

    waited = set()

    def wait_w(key):
        if key in waited or key[0] == "own" and key[2] == 0:
            return
        waited.add(key)
        if key[0] == "own":
            m = key[1]
            there = pl.ds(pl.multiple_of(dp_of(1 - zh, y, x) * blk, 16), blk)
            arrival(w.at[m, there], zsend.at[m], zrecv.at[m])
        else:
            i = index[key]
            arrival(w_slot(by_key[key], 1), wsend.at[i], wrecv.at[i])

    def t_forward(owner, ch, s):
        ref = t_slot(owner, ch)
        i = owner // NC * TCH + ch
        return ref, i

    copies[0].wait()
    for m in (K, V, Q, O):
        remote(w.at[m, mine], w.at[m, mine], zsend.at[m], zrecv.at[m], peer["zh"])
    copies[1].wait()
    copies[2].wait()

    def t_send(owner, ch, s, d):
        @pl.when((z + d >= 0) & (z + d < nz))
        def _():
            ref = t_slot(owner, ch)
            i = ((s - 1) * TCH + ch) * 2 + (d > 0)
            remote(ref, ref, tsend.at[i], trecv.at[i], {"mp": mp + d * NC}, keep=False)

    def t_share(owner, ch):
        ref = t_slot(owner, ch)
        i = owner // NC * TCH + ch
        remote(ref, ref, bsend.at[i], brecv.at[i], sibling, keep=False)

    for ch in range(TCH):
        for d in (1, -1):
            t_send(mp, ch, 1, d)
    for ch in range(TCH):
        t_share(mp, ch)

    for _, _, _, kind, what in events:
        if kind == "w":
            for key in what.needs:
                wait_w(key)
            i = index[what.key]
            ref = w_slot(what, 0)
            remote(ref, ref, wsend.at[i], wrecv.at[i], peer[what.link])
        else:
            s, ch = what
            for d in (1, -1):

                @pl.when((z - d * s >= 0) & (z - d * s < nz))
                def _():
                    owner = mp - d * s * NC
                    i = ((s - 1) * TCH + ch) * 2 + (d > 0)
                    arrival(t_slot(owner, ch), tsend.at[i], trecv.at[i])
                    if s + 1 < nz:
                        t_send(owner, ch, s + 1, d)
                    t_share(owner, ch)

    for zz in range(nz):
        for ch in range(TCH):
            owner = zz * NC + 1 - core
            i = zz * TCH + ch
            arrival(t_slot(owner, ch), bsend.at[i], brecv.at[i])
    for msg in sorted(by_key.values(), key=lambda m: when_in[m.key]):
        if msg.key[0] != O:
            wait_w(msg.key)

    d_model = n_mp * cols
    step = 64

    def norm_rows(r, _):
        at = pl.ds(pl.multiple_of(r * step, step), step)
        acc = jnp.zeros((step, cols), F32)
        for i in range(n_mp):
            v = tok[i, at, :].astype(F32)
            acc += v * v
        inv = lax.rsqrt(jnp.sum(acc, axis=1, keepdims=True) / d_model + EPS)
        for i in range(n_mp):
            gain = tok[i, pl.ds(rows, GAIN_ROWS), :].astype(F32)[0:1]
            v = tok[i, at, :].astype(F32)
            xn[at, i * cols : (i + 1) * cols] = (v * inv * gain).astype(BF16)
        return 0

    lax.fori_loop(0, rows // step, norm_rows, 0)

    def project(m, _):
        qkv[m] = jnp.dot(xn[...], w[m], preferred_element_type=F32).astype(BF16)
        return 0

    lax.fori_loop(0, 3, project, 0)

    copies[3].wait()
    part = min(128, rows)

    def attend(r, _):
        at = pl.ds(pl.multiple_of(r * part, part), part)
        for h in range(heads):
            c0, c1 = h * hd, (h + 1) * hd
            s = lax.dot_general(
                qkv[Q, at, c0:c1], qkv[K, :, c0:c1],
                (((1,), (1,)), ((), ())), preferred_element_type=F32,
            )
            s = s + bias[h, at, :].astype(F32)
            e = jnp.exp(s - jnp.max(s, axis=1, keepdims=True))
            p = (e * (1.0 / jnp.sum(e, axis=1, keepdims=True))).astype(BF16)
            ctx[at, c0:c1] = jnp.dot(
                p, qkv[V, :, c0:c1], preferred_element_type=F32
            ).astype(BF16)
        return 0

    lax.fori_loop(0, rows // part, attend, 0)

    for msg in sorted(by_key.values(), key=lambda m: when_in[m.key]):
        wait_w(msg.key)

    def out_block(zz, c):
        at = pl.ds(pl.multiple_of((zz * NC + c) * cols, cols), cols)
        return lax.dot_general(
            ctx[...], w[O, at, :], (((1,), (1,)), ((), ())), preferred_element_type=F32
        )

    near = jnp.where(z < nz // 2, 1, 0)
    sigma = 2 * near - 1
    u = jnp.where(z < nz // 2, z, nz - 1 - z)

    def real(t):
        return jnp.where(z < nz // 2, t, nz - 1 - t)

    order = []
    lo, hi = 0, nz - 1
    while lo <= hi:
        order += [hi, lo] if hi > lo else [lo]
        lo, hi = lo + 1, hi - 1
    for t in order:
        zz = real(t)
        sib_out[zz] = out_block(zz, 1 - core).astype(BF16)
        remote(sib_out.at[zz], sib_in.at[zz], psend.at[zz], precv.at[zz], sibling)
    for t in order:
        zz = real(t)
        pown[zz] = out_block(zz, core)

    rr = rows // RCH

    def chunk(ch):
        return pl.ds(ch * rr, rr)

    joined = set()

    def pair_sum(t, ch, uu):
        zz = real(t)
        if (uu, t) not in joined:
            joined.add((uu, t))
            arrival(sib_in.at[zz], psend.at[zz], precv.at[zz])
        return pown[zz, chunk(ch), :] + sib_in[zz, chunk(ch), :].astype(F32)

    def hop_in(t, ch, a):
        zz = real(t)
        way = near if a == 0 else 1 - near
        i = (way * nz + zz) * RCH + ch
        arrival(rin.at[way, zz, chunk(ch)], rsend.at[i], rrecv.at[i])
        return rin[way, zz, chunk(ch), :].astype(F32)

    def hop_out(t, ch, a, value):
        zz = real(t)
        way = near if a == 0 else 1 - near
        i = (way * nz + zz) * RCH + ch
        sout[zz, chunk(ch), :] = value.astype(BF16)
        to = mp + NC * (sigma if a == 0 else -sigma)
        remote(
            sout.at[zz, chunk(ch)], rin.at[way, zz, chunk(ch)],
            rsend.at[i], rrecv.at[i], {"mp": to}, keep=False,
        )

    hop, piece = 3.8, 5.6
    own_tok = tok.at[mp]
    for uu in range(nz // 2):

        @pl.when(u == uu)
        def _(uu=uu):
            todo = []
            for t in range(nz - 1, uu, -1):
                for ch in range(RCH):
                    at = (nz - 1 - t) * piece + uu * hop + ch * piece / RCH
                    todo.append((at, 0, t, ch))
            for t in range(uu):
                for ch in range(RCH):
                    at = t * piece + (nz - 1 - uu) * hop + ch * piece / RCH
                    todo.append((at, 1, t, ch))
            for _, a, t, ch in sorted(todo):
                value = pair_sum(t, ch, uu)
                if a == 1 or uu > 0:
                    value = value + hop_in(t, ch, a)
                hop_out(t, ch, a, value)
            for ch in range(RCH):
                value = pair_sum(uu, ch, uu) + hop_in(uu, ch, 1)
                if uu > 0:
                    value = value + hop_in(uu, ch, 0)
                value = value + own_tok[chunk(ch), :].astype(F32)
                stream_out[chunk(ch), :] = value.astype(BF16)
            for _, a, t, ch in sorted(todo):
                zz = real(t)
                way = near if a == 0 else 1 - near
                i = (way * nz + zz) * RCH + ch
                pltpu.make_async_remote_copy(
                    src_ref=sout.at[zz, chunk(ch)], dst_ref=sout.at[zz, chunk(ch)],
                    send_sem=rsend.at[i], recv_sem=rrecv.at[i],
                    device_id=sibling, device_id_type=MESH,
                ).wait_send()

    half = 128
    for r in range(rows // half):
        v = stream_out[r * half : (r + 1) * half, :].astype(F32)
        total = jnp.broadcast_to(jnp.sum(v * v, axis=1, keepdims=True), (half, 128))
        sq_in[mp, :, r * half : (r + 1) * half] = jnp.transpose(total)[0:8]
    for k in range(1, n_mp):
        other = {"mp": lax.rem(mp + k, n_mp)}
        remote(sq_in.at[mp], sq_in.at[mp], qsend.at[k], qrecv.at[k], other)
    for k in range(1, n_mp):
        source = lax.rem(mp + n_mp - k, n_mp)
        arrival(sq_in.at[source], qsend.at[k], qrecv.at[k])
    total = sq_in[0]
    for i in range(1, n_mp):
        total = total + sq_in[i]
    post = lax.rsqrt(total / d_model + EPS)
    for r in range(rows // half):
        piece_t = jnp.transpose(
            jnp.concatenate([post[:, r * half : (r + 1) * half]] * (128 // 8), axis=0)
        )
        v = stream_out[r * half : (r + 1) * half, :].astype(F32)
        scaled = v * piece_t[:, 0:1] * pgain_in[...].astype(F32)[0:1]
        normed_out[r * half : (r + 1) * half, :] = scaled.astype(BF16)

    for c in sends:
        c.wait_send()
    for s in range(1, nz):
        for ch in range(TCH):
            for d in (1, -1):
                sent = (z + d >= 0) & (z + d < nz)
                held = (z - d * (s - 1) >= 0) & (z - d * (s - 1) < nz)

                @pl.when(sent & held)
                def _():
                    ref = t_slot(mp, ch)
                    i = ((s - 1) * TCH + ch) * 2 + (d > 0)
                    pltpu.make_async_remote_copy(
                        src_ref=ref, dst_ref=ref, send_sem=tsend.at[i], recv_sem=trecv.at[i],
                        device_id=sibling, device_id_type=MESH,
                    ).wait_send()

    for zz in range(nz):
        for ch in range(TCH):
            ref = t_slot(zz * NC + core, ch)
            i = zz * TCH + ch
            pltpu.make_async_remote_copy(
                src_ref=ref, dst_ref=ref, send_sem=bsend.at[i], recv_sem=brecv.at[i],
                device_id=sibling, device_id_type=MESH,
            ).wait_send()


def on_device(tokens, pre_gain, input_weight, output_weight, position_bias, post_gain):
    rows, cols = tokens.shape
    blk = input_weight.shape[1]
    n_mp = lax.axis_size("mp")
    n_dp = lax.axis_size("dp")
    nz = n_mp // NC
    heads, seq, _ = position_bias.shape
    wide = jnp.concatenate([input_weight, output_weight.T[None]], axis=0)
    gain = jnp.broadcast_to(pre_gain[None], (GAIN_ROWS, cols))
    pgain = jnp.broadcast_to(post_gain[None], (8, cols))
    n_msgs = len(weight_messages())
    any_spec = pl.BlockSpec(memory_space=pl.ANY)
    vmem = pl.BlockSpec(memory_space=pltpu.VMEM)
    dma = pltpu.SemaphoreType.DMA
    return pl.pallas_call(
        functools.partial(body, nz),
        out_shape=(
            jax.ShapeDtypeStruct((rows, cols), BF16),
            jax.ShapeDtypeStruct((rows, cols), BF16),
        ),
        in_specs=[any_spec, any_spec, any_spec, any_spec, vmem],
        out_specs=(vmem, vmem),
        scratch_shapes=[
            pltpu.VMEM((n_mp, rows + GAIN_ROWS, cols), BF16),
            pltpu.VMEM((4, n_dp * blk, cols), BF16),
            pltpu.VMEM((heads, seq, seq), BF16),
            pltpu.VMEM((rows, n_mp * cols), BF16),
            pltpu.VMEM((3, rows, cols), BF16),
            pltpu.VMEM((rows, cols), BF16),
            pltpu.VMEM((nz, rows, cols), F32),
            pltpu.VMEM((nz, rows, cols), BF16),
            pltpu.VMEM((nz, rows, cols), BF16),
            pltpu.VMEM((2, nz, rows, cols), BF16),
            pltpu.VMEM((nz, rows, cols), BF16),
            pltpu.VMEM((n_mp, 8, rows), F32),
            dma((4,)),
            dma((n_msgs,)),
            dma((n_msgs,)),
            dma((4,)),
            dma((4,)),
            dma((2 * TCH * (nz - 1),)),
            dma((2 * TCH * (nz - 1),)),
            dma((nz * TCH,)),
            dma((nz * TCH,)),
            dma((nz,)),
            dma((nz,)),
            dma((2 * nz * RCH,)),
            dma((2 * nz * RCH,)),
            dma((n_mp,)),
            dma((n_mp,)),
        ],
        compiler_params=pltpu.CompilerParams(
            collective_id=0, has_side_effects=True, vmem_limit_bytes=62 * 1024 * 1024
        ),
    )(tokens, gain, wide, position_bias, pgain)


def solution(mesh):
    return jax.shard_map(
        on_device,
        mesh=mesh,
        in_specs=(
            P("dp", "mp"),
            P("mp"),
            P(None, "dp", "mp"),
            P("mp", "dp"),
            P("mp", None, None),
            P("mp"),
        ),
        out_specs=(P("dp", "mp"), P("dp", "mp")),
        check_vma=False,
    )
```

time: 431 us -> 148 us (0.34)
  waiting for transfers between devices: 337 us -> 0 us
  Pallas kernels: 0 us -> 140 us
  blocking collectives: 30.1 us -> 0 us
  matrix products: 15.8 us -> 0 us
  between operations: 13.8 us -> 0.64 us
  local copies, waits for them, and re-layouts: 18.1 us -> 5.83 us
  starting transfers between devices: 9.11 us -> 0 us
  other arithmetic: 6.04 us -> 1.55 us
    all_gather x2 -> x0, waiting for transfers between devices: 258 us -> none  [the longest x1 217 us: gather_turned(): lax.all_gather(both, axis, axis=0, tiled=True)]
    pallas_call x0 -> x1, Pallas kernels: none -> 140 us  [on_device(): pl.pallas_call(functools.partial(body, nz), out_shape=(jax.ShapeDtypeStru...]
    reduce_scatter x1 -> x0, waiting for transfers between devices: 70.3 us -> none  [on_device(): lax.psum_scatter(partial_value.astype(jnp.bfloat16), 'mp', scatter_dimens...]
    all_gather x1 -> x0, blocking collectives: 30.1 us -> none  [on_device(): lax.all_gather(pre_gain, 'mp', axis=0, tiled=True)]
    dot_general x3 -> x0, matrix products: 12.7 us -> none  [the longest x1 5.04 us: on_device(): jnp.einsum('td,kdi->kti', normed_in, input_full, preferred_element_type=j...]
    slice x3 -> x0, local copies, waits for them, and re-layouts: 11.8 us -> none  [the longest x2 11.7 us: gather_turned(): slab = whole[:, at:at + t[0].size].reshape(-1, *t.shape[1:])]
    all_to_all x1 -> x0, starting transfers between devices: 8.99 us -> none  [copy_for_each(): lax.all_to_all(jnp.broadcast_to(array[None], (size, *array.shape)), axis,...]
    all_to_all x1 -> x0, waiting for transfers between devices: 8.36 us -> none  [copy_for_each(): lax.all_to_all(jnp.broadcast_to(array[None], (size, *array.shape)), axis,...]
  transfers between devices with their start and end apart: 4 -> 0, of which waited for: 4 -> 0; matrix products, arithmetic and copies ran while one was open for 2% -> 0% of each run, Pallas kernels for 0% -> 0%
where the time goes in v1:
time: 148 us
  Pallas kernels  140 us (95%)
  local copies, waits for them, and re-layouts  5.83 us (4%)
  other arithmetic  1.55 us (1%)
    pallas_call x1, Pallas kernels, on_device(): pl.pallas_call(functools.partial(body, nz), out_shape=(jax.ShapeDtypeStru...  140 us
    unnamed x2, local copies, waits for them, and re-layouts  3.34 us

profile of v1, /device:TPU:1, one launch (start us, length us, event | category | flops | bytes accessed | tf_op | source)
XLA Modules:
  0.0 148.1 jit_solution(7440314631306042236)
XLA Ops:
  0.6 1.2 broadcast_in_dim.8.pgain_in
  1.9 1.3 broadcast_in_dim.6.gain_in
  3.1 1.6 %pad_maximum_fusion.w_in = bf16[4,48,256]{2,1,0:T(8,128)(2,1)} fusion(bf16[1,48,256]{2,1,0:T(8,128)(2,1)} %bitcast.3, bf16[3,48,256]{2,1,0:T(8,128)(2,1)} %param.8), kind=kLoop, calls=%fused_computation | loop fusion | flops 49152 | bytes 196608 | tf_op jit(solution)/shard_map/concatenate | solution.py:474
  4.7 140.1 %shard_map.77 = (bf16[512,256]{1,0:T(8,128)(2,1)}, bf16[512,256]{1,0:T(8,128)(2,1)}) custom-call(bf16[512,256]{1,0:T(8,128)(2,1)} %tok_in.1, bf16[16,256]{1,0:T(8,128)(2,1)} %broadcast_in_dim.6.gain_in, bf16[4,48,256]{2,1,0:T(8,128)(2,1)} %pad_maximum_fusion.w_in, bf16[4,512,512]{2,1,0:T(8,128)(2,1)} %bias_in.1, bf16[8,256]{1,0:T(8,128)(2,1)} %broadcast_in_dim.8.pgain_in), custom_call_target="tpu_custom_call" | custom-call | tf_op jit(solution)/shard_map/pallas_call | solution.py:481
  144.8 1.7 %copy.10 = bf16[512,256]{1,0:T(8,128)(2,1)} copy(bf16[512,256]{1,0:T(8,128)(2,1)} %get-tuple-element.4) | data formatting | bytes 524288
  146.5 1.7 %copy.11 = bf16[512,256]{1,0:T(8,128)(2,1)} copy(bf16[512,256]{1,0:T(8,128)(2,1)} %get-tuple-element.5) | data formatting | bytes 524288

commit v2 on v1

--- a/solution.py
+++ b/solution.py
@@ -19,6 +19,7 @@
 SPLIT = 2
 TCH = 2
 RCH = 4
+LATE_START = 20.0
 
 
 class Msg:
@@ -67,39 +68,59 @@
     return msgs
 
 
-def weight_schedule(arrivals, rate=46650.0, latency=2.2, unit=24576):
+def weight_schedule(arrivals, rate=46650.0, latency=2.4, unit=24576):
+    msgs = weight_messages()
+    tail = {}
+    for msg in reversed(msgs):
+        mine = msg.size * unit / rate + latency + tail.get(msg.key, 0.0)
+        for n in msg.needs:
+            tail[n] = max(tail.get(n, 0.0), mine)
     avail = dict(arrivals)
-    pending = weight_messages()
     free = {"x+": 0.0, "x-": 0.0, "y+": 0.0, "y-": 0.0}
     out = []
+    pending = list(msgs)
     while pending:
         best = None
         for msg in pending:
             if all(n in avail for n in msg.needs):
                 ready = max(avail[n] for n in msg.needs)
-                late = 1 if msg.key[0] == O else 0
-                cand = (max(ready, free[msg.link]) + 3.0 * late, msg.rank, ready)
-                if best is None or cand[:2] < best[0][:2]:
+                rank = -tail.get(msg.key, 0.0)
+                if msg.key[0] == O:
+                    rank += 100.0
+                    if msg.key[2] == "Y":
+                        ready = max(ready, LATE_START)
+                cand = (max(ready, free[msg.link]), rank, msg.rank)
+                if best is None or cand < best[0]:
                     best = (cand, msg)
-        (_, _, ready), msg = best
+        (start, _, _), msg = best
         pending.remove(msg)
-        start = max(ready, free[msg.link])
         end = start + msg.size * unit / rate
         free[msg.link] = end
         avail[msg.key] = end + latency
         out.append((start, msg))
+    out.sort(key=lambda e: (e[0], e[1].rank))
     return out, avail
 
 
 def body(
-    nz, tok_in, gain_in, w_in, bias_in, pgain_in, stream_out, normed_out,
+    nz, tok_in, gain_in, wi_in, wo_in, bias_in, pgain_in, stream_out, normed_out,
     tok, w, bias, xn, qkv, ctx, pown, sib_out, sib_in, rin, sout, sq_in,
     loc_sem, wsend, wrecv, zsend, zrecv, tsend, trecv, bsend, brecv,
     psend, precv, rsend, rrecv, qsend, qrecv,
 ):
     rows, cols = tok_in.shape
-    blk = w_in.shape[1]
+    blk = wi_in.shape[1]
     dp, mp = lax.axis_index("dp"), lax.axis_index("mp")
+    opened = []
+
+    def mark(name):
+        while opened:
+            opened.pop().__exit__(None, None, None)
+        if name:
+            opened.append(jax.named_scope(name))
+            opened[-1].__enter__()
+
+    mark("entry")
     x = lax.rem(dp, NX)
     y = lax.rem(dp // NX, NY)
     zh = dp // (NX * NY)
@@ -126,9 +147,9 @@
 
     mine = pl.ds(pl.multiple_of(dp * blk, 16), blk)
     copies = [
-        pltpu.make_async_copy(w_in, w.at[:, mine], loc_sem.at[0]),
+        pltpu.make_async_copy(wi_in, w.at[pl.ds(0, 3), mine], loc_sem.at[0]),
         pltpu.make_async_copy(tok_in, tok.at[mp, pl.ds(0, rows)], loc_sem.at[1]),
-        pltpu.make_async_copy(gain_in, tok.at[mp, pl.ds(rows, GAIN_ROWS)], loc_sem.at[2]),
+        pltpu.make_async_copy(wo_in, w.at[O, mine], loc_sem.at[2]),
         pltpu.make_async_copy(bias_in, bias, loc_sem.at[3]),
     ]
     for c in copies:
@@ -140,6 +161,16 @@
     for k in range(1, n_mp):
         other = {"mp": lax.rem(mp + k, n_mp)}
         pl.semaphore_signal(barrier, inc=1, device_id=other, device_id_type=MESH)
+    tok[mp, rows : rows + GAIN_ROWS, :] = jnp.broadcast_to(
+        gain_in[...].astype(F32).reshape(1, cols), (GAIN_ROWS, cols)
+    ).astype(BF16)
+    copies[2].wait()
+    copies[0].wait()
+    copies[1].wait()
+    for g in range(cols // min(128, cols)):
+        half_l = min(128, cols)
+        qkv[V, g, :, half_l:] = jnp.ones((rows, half_l), BF16)
+        ctx[g] = jnp.zeros((rows, half_l), BF16)
     pl.semaphore_wait(barrier, len(peer) + n_mp - 1)
 
     sends = []
@@ -189,15 +220,17 @@
     for m in (Q, K, V, O):
         arrivals["own", m, 0] = T0
     for i, m in enumerate((K, V, Q, O)):
-        arrivals["own", m, 1] = T0 + 8.0 + i
+        arrivals["own", m, 1] = T0 + 7.0 + 0.7 * i
     schedule, when_in = weight_schedule(arrivals)
     index = {msg.key: i for i, (_, msg) in enumerate(schedule)}
     by_key = {msg.key: msg for _, msg in schedule}
+    in_order = sorted(by_key, key=lambda k: when_in[k])
     events = [(t, 1, i, "w", msg) for i, (t, msg) in enumerate(schedule)]
     for s in range(1, nz):
         for ch in range(TCH):
-            t = T0 + 2.0 + 5.8 * (s * TCH + ch + 1 - TCH) / TCH + 1.0
+            t = T0 + 3.5 + 5.8 * (s * TCH + ch + 1 - TCH) / TCH
             events.append((t, 0, s * TCH + ch, "t", (s, ch)))
+    t_tokens = max(e[0] for e in events if e[3] == "t") + 1.5
     events.sort(key=lambda e: e[:3])
 
     waited = set()
@@ -214,17 +247,6 @@
             i = index[key]
             arrival(w_slot(by_key[key], 1), wsend.at[i], wrecv.at[i])
 
-    def t_forward(owner, ch, s):
-        ref = t_slot(owner, ch)
-        i = owner // NC * TCH + ch
-        return ref, i
-
-    copies[0].wait()
-    for m in (K, V, Q, O):
-        remote(w.at[m, mine], w.at[m, mine], zsend.at[m], zrecv.at[m], peer["zh"])
-    copies[1].wait()
-    copies[2].wait()
-
     def t_send(owner, ch, s, d):
         @pl.when((z + d >= 0) & (z + d < nz))
         def _():
@@ -237,43 +259,39 @@
         i = owner // NC * TCH + ch
         remote(ref, ref, bsend.at[i], brecv.at[i], sibling, keep=False)
 
-    for ch in range(TCH):
-        for d in (1, -1):
-            t_send(mp, ch, 1, d)
-    for ch in range(TCH):
-        t_share(mp, ch)
-
-    for _, _, _, kind, what in events:
+    def run_event(kind, what):
         if kind == "w":
             for key in what.needs:
-                wait_w(key)
+                with jax.named_scope("w_" + "_".join(str(v) for v in key)):
+                    wait_w(key)
             i = index[what.key]
             ref = w_slot(what, 0)
             remote(ref, ref, wsend.at[i], wrecv.at[i], peer[what.link])
-        else:
-            s, ch = what
-            for d in (1, -1):
-
-                @pl.when((z - d * s >= 0) & (z - d * s < nz))
-                def _():
-                    owner = mp - d * s * NC
-                    i = ((s - 1) * TCH + ch) * 2 + (d > 0)
+            return
+        s, ch = what
+        for d in (1, -1):
+
+            @pl.when((z - d * s >= 0) & (z - d * s < nz))
+            def _(d=d):
+                owner = mp - d * s * NC
+                i = ((s - 1) * TCH + ch) * 2 + (d > 0)
+                with jax.named_scope("t_%d_%d_%d" % (s, ch, d)):
                     arrival(t_slot(owner, ch), tsend.at[i], trecv.at[i])
-                    if s + 1 < nz:
-                        t_send(owner, ch, s + 1, d)
-                    t_share(owner, ch)
-
-    for zz in range(nz):
-        for ch in range(TCH):
-            owner = zz * NC + 1 - core
-            i = zz * TCH + ch
-            arrival(t_slot(owner, ch), bsend.at[i], brecv.at[i])
-    for msg in sorted(by_key.values(), key=lambda m: when_in[m.key]):
-        if msg.key[0] != O:
-            wait_w(msg.key)
+                if s + 1 < nz:
+                    t_send(owner, ch, s + 1, d)
+                t_share(owner, ch)
 
     d_model = n_mp * cols
-    step = 64
+    step = min(64, rows)
+    part = min(512, rows)
+    n_part = rows // part
+
+    def tokens_done():
+        for zz in range(nz):
+            for ch in range(TCH):
+                owner = zz * NC + 1 - core
+                i = zz * TCH + ch
+                arrival(t_slot(owner, ch), bsend.at[i], brecv.at[i])
 
     def norm_rows(r, _):
         at = pl.ds(pl.multiple_of(r * step, step), step)
@@ -288,42 +306,94 @@
             xn[at, i * cols : (i + 1) * cols] = (v * inv * gain).astype(BF16)
         return 0
 
-    lax.fori_loop(0, rows // step, norm_rows, 0)
-
-    def project(m, _):
-        qkv[m] = jnp.dot(xn[...], w[m], preferred_element_type=F32).astype(BF16)
+    def norm_part(p):
+        per = 128 // step
+        lax.fori_loop(p * per, (p + 1) * per, norm_rows, 0)
+
+    def project():
+        for key in in_order:
+            if key[0] != O:
+                wait_w(key)
+
+        def one(m, _):
+            r = jnp.dot(xn[...], w[m], preferred_element_type=F32).astype(BF16)
+            for g in range(groups):
+                qkv[m, g, :, 0:lanes] = r[:, g * lanes : (g + 1) * lanes]
+            return 0
+
+        lax.fori_loop(0, 3, one, 0)
+
+    lanes = min(128, cols)
+    groups = cols // lanes
+    per = lanes // hd
+
+    def attend_one(i, _):
+        h = lax.rem(i, heads)
+        at = pl.ds(pl.multiple_of(i // heads * part, part), part)
+        g = h // per
+        first = lax.rem(h, per) * hd
+        lane = lax.broadcasted_iota(jnp.int32, (part, lanes), 1)
+        mine_l = (lane >= first) & (lane < first + hd)
+        q = jnp.where(mine_l, qkv[Q, g, at, 0:lanes], jnp.zeros((), BF16))
+        s = lax.dot_general(
+            q, qkv[K, g, :, 0:lanes],
+            (((1,), (1,)), ((), ())), preferred_element_type=F32,
+        )
+        s = s + bias[h, at, :].astype(F32)
+        e = jnp.exp(s - jnp.max(s, axis=1, keepdims=True)).astype(BF16)
+        o = jnp.dot(e, qkv[V, g], preferred_element_type=F32)
+        o = (o[:, 0:lanes] * (1.0 / o[:, lanes:])).astype(BF16)
+        ctx[g, at, :] = jnp.where(mine_l, o, ctx[g, at, :])
         return 0
 
-    lax.fori_loop(0, 3, project, 0)
-
-    copies[3].wait()
-    part = min(128, rows)
-
-    def attend(r, _):
-        at = pl.ds(pl.multiple_of(r * part, part), part)
-        for h in range(heads):
-            c0, c1 = h * hd, (h + 1) * hd
-            s = lax.dot_general(
-                qkv[Q, at, c0:c1], qkv[K, :, c0:c1],
-                (((1,), (1,)), ((), ())), preferred_element_type=F32,
-            )
-            s = s + bias[h, at, :].astype(F32)
-            e = jnp.exp(s - jnp.max(s, axis=1, keepdims=True))
-            p = (e * (1.0 / jnp.sum(e, axis=1, keepdims=True))).astype(BF16)
-            ctx[at, c0:c1] = jnp.dot(
-                p, qkv[V, :, c0:c1], preferred_element_type=F32
-            ).astype(BF16)
-        return 0
-
-    lax.fori_loop(0, rows // part, attend, 0)
-
-    for msg in sorted(by_key.values(), key=lambda m: when_in[m.key]):
-        wait_w(msg.key)
+    def attend(i):
+        lax.fori_loop(2 * i, 2 * i + 2, attend_one, 0)
+
+    t_of = {m: max(when_in[k] for k in in_order if k[0] == m) for m in (Q, K, V)}
+    t_proj = max(list(t_of.values()) + [t_tokens])
+    steps = [(t_tokens, 0.02, "tokens", tokens_done)]
+    for p in range(rows // 128):
+        steps.append((t_tokens, 0.37, "norm_in", functools.partial(norm_part, p)))
+    steps.append((t_proj, 2.9, "project", project))
+    steps.append((t_proj, 0.0, "bias", copies[3].wait))
+    for i in range(n_part * heads // 2):
+        steps.append((t_proj, 1.6, "attend", functools.partial(attend, i)))
+
+    mark("first")
+    while events[0][3] == "w" and events[0][0] < T0 + 0.1:
+        run_event(*events.pop(0)[3:])
+    for m in (K, V, Q, O):
+        remote(w.at[m, mine], w.at[m, mine], zsend.at[m], zrecv.at[m], peer["zh"])
+    mark(None)
+    now = T0
+    late_sends = 4
+    while events or steps:
+        late_sends -= 1
+        if late_sends == 0:
+            for ch in range(TCH):
+                for d in (1, -1):
+                    t_send(mp, ch, 1, d)
+            for ch in range(TCH):
+                t_share(mp, ch)
+        if events and (events[0][0] <= now or not steps):
+            run_event(*events.pop(0)[3:])
+        elif steps and steps[0][0] <= now:
+            _, cost, name, call = steps.pop(0)
+            with jax.named_scope(name):
+                call()
+            now += cost
+        else:
+            now = min(e[0][0] for e in (events, steps) if e)
+
+    mark("owait")
+    for key in in_order:
+        wait_w(key)
 
     def out_block(zz, c):
         at = pl.ds(pl.multiple_of((zz * NC + c) * cols, cols), cols)
+        whole = jnp.concatenate([ctx[g] for g in range(groups)], axis=1)
         return lax.dot_general(
-            ctx[...], w[O, at, :], (((1,), (1,)), ((), ())), preferred_element_type=F32
+            whole, w[O, at, :], (((1,), (1,)), ((), ())), preferred_element_type=F32
         )
 
     near = jnp.where(z < nz // 2, 1, 0)
@@ -333,6 +403,7 @@
     def real(t):
         return jnp.where(z < nz // 2, t, nz - 1 - t)
 
+    mark("outproj")
     order = []
     lo, hi = 0, nz - 1
     while lo <= hi:
@@ -342,10 +413,6 @@
         zz = real(t)
         sib_out[zz] = out_block(zz, 1 - core).astype(BF16)
         remote(sib_out.at[zz], sib_in.at[zz], psend.at[zz], precv.at[zz], sibling)
-    for t in order:
-        zz = real(t)
-        pown[zz] = out_block(zz, core)
-
     rr = rows // RCH
 
     def chunk(ch):
@@ -357,6 +424,7 @@
         zz = real(t)
         if (uu, t) not in joined:
             joined.add((uu, t))
+            pown[zz] = out_block(zz, core)
             arrival(sib_in.at[zz], psend.at[zz], precv.at[zz])
         return pown[zz, chunk(ch), :] + sib_in[zz, chunk(ch), :].astype(F32)
 
@@ -378,6 +446,7 @@
             rsend.at[i], rrecv.at[i], {"mp": to}, keep=False,
         )
 
+    mark("reduce")
     hop, piece = 3.8, 5.6
     own_tok = tok.at[mp]
     for uu in range(nz // 2):
@@ -393,17 +462,24 @@
                 for ch in range(RCH):
                     at = t * piece + (nz - 1 - uu) * hop + ch * piece / RCH
                     todo.append((at, 1, t, ch))
-            for _, a, t, ch in sorted(todo):
+            moves = list(todo)
+            for ch in range(RCH):
+                at = (nz - 1 - uu) * hop + uu * piece + (ch + 1) * piece / RCH
+                if uu > 0:
+                    at = max(at, (nz - uu) * piece + hop + ch * piece / RCH)
+                moves.append((at, 2, uu, ch))
+            for _, a, t, ch in sorted(moves):
                 value = pair_sum(t, ch, uu)
+                if a == 2:
+                    value = value + hop_in(t, ch, 1)
+                    if uu > 0:
+                        value = value + hop_in(t, ch, 0)
+                    value = value + own_tok[chunk(ch), :].astype(F32)
+                    stream_out[chunk(ch), :] = value.astype(BF16)
+                    continue
                 if a == 1 or uu > 0:
                     value = value + hop_in(t, ch, a)
                 hop_out(t, ch, a, value)
-            for ch in range(RCH):
-                value = pair_sum(uu, ch, uu) + hop_in(uu, ch, 1)
-                if uu > 0:
-                    value = value + hop_in(uu, ch, 0)
-                value = value + own_tok[chunk(ch), :].astype(F32)
-                stream_out[chunk(ch), :] = value.astype(BF16)
             for _, a, t, ch in sorted(todo):
                 zz = real(t)
                 way = near if a == 0 else 1 - near
@@ -414,6 +490,7 @@
                     device_id=sibling, device_id_type=MESH,
                 ).wait_send()
 
+    mark("squares")
     half = 128
     for r in range(rows // half):
         v = stream_out[r * half : (r + 1) * half, :].astype(F32)
@@ -421,22 +498,24 @@
         sq_in[mp, :, r * half : (r + 1) * half] = jnp.transpose(total)[0:8]
     for k in range(1, n_mp):
         other = {"mp": lax.rem(mp + k, n_mp)}
-        remote(sq_in.at[mp], sq_in.at[mp], qsend.at[k], qrecv.at[k], other)
+        remote(sq_in.at[mp, pl.ds(0, 1)], sq_in.at[mp, pl.ds(0, 1)], qsend.at[k], qrecv.at[k], other)
     for k in range(1, n_mp):
         source = lax.rem(mp + n_mp - k, n_mp)
-        arrival(sq_in.at[source], qsend.at[k], qrecv.at[k])
-    total = sq_in[0]
+        arrival(sq_in.at[source, pl.ds(0, 1)], qsend.at[k], qrecv.at[k])
+    mark("final")
+    total = sq_in[0, 0:1, :]
     for i in range(1, n_mp):
-        total = total + sq_in[i]
+        total = total + sq_in[i, 0:1, :]
     post = lax.rsqrt(total / d_model + EPS)
     for r in range(rows // half):
         piece_t = jnp.transpose(
-            jnp.concatenate([post[:, r * half : (r + 1) * half]] * (128 // 8), axis=0)
+            jnp.broadcast_to(post[:, r * half : (r + 1) * half], (128, half))
         )
         v = stream_out[r * half : (r + 1) * half, :].astype(F32)
-        scaled = v * piece_t[:, 0:1] * pgain_in[...].astype(F32)[0:1]
+        scaled = v * piece_t[:, 0:1] * pgain_in[...].astype(F32).reshape(1, cols)
         normed_out[r * half : (r + 1) * half, :] = scaled.astype(BF16)
 
+    mark("drain")
     for c in sends:
         c.wait_send()
     for s in range(1, nz):
@@ -463,6 +542,8 @@
                 device_id=sibling, device_id_type=MESH,
             ).wait_send()
 
+    mark(None)
+
 
 def on_device(tokens, pre_gain, input_weight, output_weight, position_bias, post_gain):
     rows, cols = tokens.shape
@@ -471,10 +552,8 @@
     n_dp = lax.axis_size("dp")
     nz = n_mp // NC
     heads, seq, _ = position_bias.shape
-    wide = jnp.concatenate([input_weight, output_weight.T[None]], axis=0)
-    gain = jnp.broadcast_to(pre_gain[None], (GAIN_ROWS, cols))
-    pgain = jnp.broadcast_to(post_gain[None], (8, cols))
     n_msgs = len(weight_messages())
+    lanes = min(128, cols)
     any_spec = pl.BlockSpec(memory_space=pl.ANY)
     vmem = pl.BlockSpec(memory_space=pltpu.VMEM)
     dma = pltpu.SemaphoreType.DMA
@@ -484,15 +563,15 @@
             jax.ShapeDtypeStruct((rows, cols), BF16),
             jax.ShapeDtypeStruct((rows, cols), BF16),
         ),
-        in_specs=[any_spec, any_spec, any_spec, any_spec, vmem],
+        in_specs=[any_spec, vmem, any_spec, any_spec, any_spec, vmem],
         out_specs=(vmem, vmem),
         scratch_shapes=[
             pltpu.VMEM((n_mp, rows + GAIN_ROWS, cols), BF16),
             pltpu.VMEM((4, n_dp * blk, cols), BF16),
             pltpu.VMEM((heads, seq, seq), BF16),
             pltpu.VMEM((rows, n_mp * cols), BF16),
-            pltpu.VMEM((3, rows, cols), BF16),
-            pltpu.VMEM((rows, cols), BF16),
+            pltpu.VMEM((3, cols // lanes, rows, 2 * lanes), BF16),
+            pltpu.VMEM((cols // lanes, rows, lanes), BF16),
             pltpu.VMEM((nz, rows, cols), F32),
             pltpu.VMEM((nz, rows, cols), BF16),
             pltpu.VMEM((nz, rows, cols), BF16),
@@ -518,7 +597,7 @@
         compiler_params=pltpu.CompilerParams(
             collective_id=0, has_side_effects=True, vmem_limit_bytes=62 * 1024 * 1024
         ),
-    )(tokens, gain, wide, position_bias, pgain)
+    )(tokens, pre_gain, input_weight, output_weight.T, position_bias, post_gain)
 
 
 def solution(mesh):

time: 148 us -> 123 us (0.83)
  Pallas kernels: 140 us -> 119 us
  local copies, waits for them, and re-layouts: 5.83 us -> 3.34 us
  other arithmetic: 1.55 us -> 0 us
    pallas_call x1, Pallas kernels: 140 us -> 119 us  [on_device(): pl.pallas_call(functools.partial(body, nz), out_shape=(jax.ShapeDtypeStru...]
    broadcast_in_dim x2 -> x0, local copies, waits for them, and re-layouts: 2.5 us -> none  [the longest x1 1.26 us: on_device(): gain = jnp.broadcast_to(pre_gain[None], (GAIN_ROWS, cols))]
    concatenate x1 -> x0, other arithmetic: 1.55 us -> none  [on_device(): wide = jnp.concatenate([input_weight, output_weight.T[None]], axis=0)]
where the time goes in v2:
time: 123 us
  Pallas kernels  119 us (97%)
  local copies, waits for them, and re-layouts  3.34 us (3%)
    pallas_call x1, Pallas kernels, on_device(): pl.pallas_call(functools.partial(body, nz), out_shape=(jax.ShapeDtypeStru...  119 us
    unnamed x2, local copies, waits for them, and re-layouts  3.34 us

profile of v2, /device:TPU:1, one launch (start us, length us, event | category | flops | bytes accessed | tf_op | source)
XLA Modules:
  0.0 123.2 jit_solution(10356866910445327895)
XLA Ops:
  0.6 119.2 %shard_map.77 = (bf16[512,256]{1,0:T(8,128)(2,1)}, bf16[512,256]{1,0:T(8,128)(2,1)}) custom-call(bf16[512,256]{1,0:T(8,128)(2,1)} %tok_in.1, bf16[256]{0:T(256)(128)(2,1)} %gain_in.1, bf16[3,48,256]{2,1,0:T(8,128)(2,1)} %wi_in.1, bf16[48,256]{1,0:T(8,128)(2,1)} %bitcast.1, bf16[4,512,512]{2,1,0:T(8,128)(2,1)} %bias_in.1, bf16[256]{0:T(256)(128)(2,1)} %pgain_in.1), custom_call_target="tpu_custom_call" | custom-call | tf_op jit(solution)/shard_map/pallas_call | solution.py:560
  119.8 1.7 %copy.10 = bf16[512,256]{1,0:T(8,128)(2,1)} copy(bf16[512,256]{1,0:T(8,128)(2,1)} %get-tuple-element.4) | data formatting | bytes 524288
  121.5 1.7 %copy.11 = bf16[512,256]{1,0:T(8,128)(2,1)} copy(bf16[512,256]{1,0:T(8,128)(2,1)} %get-tuple-element.5) | data formatting | bytes 524288

commit v3 on v2

--- a/solution.py
+++ b/solution.py
@@ -11,7 +11,7 @@
 MESH = pl.DeviceIdType.MESH
 F32 = jnp.float32
 BF16 = jnp.bfloat16
-GAIN_ROWS = 16
+GAIN_ROWS = 8
 NH, NY, NX = 2, 8, 4
 NC = 2
 Q, K, V, O = 0, 1, 2, 3
@@ -19,7 +19,9 @@
 SPLIT = 2
 TCH = 2
 RCH = 4
-LATE_START = 20.0
+LATE_START = 0.0
+FIRST_LATE = 2.5
+LATE_RANK = 8.0
 
 
 class Msg:
@@ -68,7 +70,7 @@
     return msgs
 
 
-def weight_schedule(arrivals, rate=46650.0, latency=2.4, unit=24576):
+def weight_schedule(arrivals, rate=46650.0, latency=2.6, unit=24576):
     msgs = weight_messages()
     tail = {}
     for msg in reversed(msgs):
@@ -86,7 +88,7 @@
                 ready = max(avail[n] for n in msg.needs)
                 rank = -tail.get(msg.key, 0.0)
                 if msg.key[0] == O:
-                    rank += 100.0
+                    rank += LATE_RANK
                     if msg.key[2] == "Y":
                         ready = max(ready, LATE_START)
                 cand = (max(ready, free[msg.link]), rank, msg.rank)
@@ -96,16 +98,16 @@
         pending.remove(msg)
         end = start + msg.size * unit / rate
         free[msg.link] = end
-        avail[msg.key] = end + latency
+        avail[msg.key] = end + latency + (FIRST_LATE if msg.needs[0][0::2] == ("own", 0) else 0.0)
         out.append((start, msg))
     out.sort(key=lambda e: (e[0], e[1].rank))
     return out, avail
 
 
 def body(
-    nz, tok_in, gain_in, wi_in, wo_in, bias_in, pgain_in, stream_out, normed_out,
+    nz, tok_in, gain_in, wi_in, wo_in, bias_in, pgain_in, attn_out, scale_out,
     tok, w, bias, xn, qkv, ctx, pown, sib_out, sib_in, rin, sout, sq_in,
-    loc_sem, wsend, wrecv, zsend, zrecv, tsend, trecv, bsend, brecv,
+    loc_sem, in_sem, wsend, wrecv, zsend, zrecv, tsend, trecv, bsend, brecv,
     psend, precv, rsend, rrecv, qsend, qrecv,
 ):
     rows, cols = tok_in.shape
@@ -156,8 +158,14 @@
         c.start()
 
     barrier = pltpu.get_barrier_semaphore()
-    for p in peer.values():
-        pl.semaphore_signal(barrier, inc=1, device_id=p, device_id_type=MESH)
+    for k, p in peer.items():
+        if k != "zh":
+            pl.semaphore_signal(barrier, inc=1, device_id=p, device_id_type=MESH)
+
+    @pl.when(zh == 0)
+    def _():
+        pl.semaphore_signal(barrier, inc=1, device_id=peer["zh"], device_id_type=MESH)
+
     for k in range(1, n_mp):
         other = {"mp": lax.rem(mp + k, n_mp)}
         pl.semaphore_signal(barrier, inc=1, device_id=other, device_id_type=MESH)
@@ -171,7 +179,7 @@
         half_l = min(128, cols)
         qkv[V, g, :, half_l:] = jnp.ones((rows, half_l), BF16)
         ctx[g] = jnp.zeros((rows, half_l), BF16)
-    pl.semaphore_wait(barrier, len(peer) + n_mp - 1)
+    pl.semaphore_wait(barrier, len(peer) - 1 + n_mp - 1 + zh)
 
     sends = []
 
@@ -190,6 +198,12 @@
             src_ref=ref, dst_ref=ref, send_sem=ssem, recv_sem=rsem,
             device_id=sibling, device_id_type=MESH,
         ).wait_recv()
+
+    def sent_off(ref, ssem, rsem):
+        pltpu.make_async_remote_copy(
+            src_ref=ref, dst_ref=ref, send_sem=ssem, recv_sem=rsem,
+            device_id=sibling, device_id_type=MESH,
+        ).wait_send()
 
     def w_slot(msg, back):
         m, half, kind, g, s, d = msg.key
@@ -210,17 +224,18 @@
                 row = dp_of(h, wrap(y + g, NY), wrap(x - hop, NX))
         return w.at[m, pl.ds(pl.multiple_of(row * blk, 16), n * blk)]
 
-    crow = (rows + GAIN_ROWS) // TCH
+    crow = rows // TCH
 
     def t_slot(owner, ch):
-        return tok.at[owner, pl.ds(ch * crow, crow)]
+        n = crow + (GAIN_ROWS if ch == TCH - 1 else 0)
+        return tok.at[owner, pl.ds(ch * crow, n)]
 
     T0 = 1.5
     arrivals = {}
     for m in (Q, K, V, O):
         arrivals["own", m, 0] = T0
     for i, m in enumerate((K, V, Q, O)):
-        arrivals["own", m, 1] = T0 + 7.0 + 0.7 * i
+        arrivals["own", m, 1] = T0 + 9.5 + 0.7 * i
     schedule, when_in = weight_schedule(arrivals)
     index = {msg.key: i for i, (_, msg) in enumerate(schedule)}
     by_key = {msg.key: msg for _, msg in schedule}
@@ -228,7 +243,7 @@
     events = [(t, 1, i, "w", msg) for i, (t, msg) in enumerate(schedule)]
     for s in range(1, nz):
         for ch in range(TCH):
-            t = T0 + 3.5 + 5.8 * (s * TCH + ch + 1 - TCH) / TCH
+            t = 13.0 + 5.8 * (s - 1) + 2.9 * ch if s > 1 else 9.0 + 2.9 * ch
             events.append((t, 0, s * TCH + ch, "t", (s, ch)))
     t_tokens = max(e[0] for e in events if e[3] == "t") + 1.5
     events.sort(key=lambda e: e[:3])
@@ -260,6 +275,9 @@
         remote(ref, ref, bsend.at[i], brecv.at[i], sibling, keep=False)
 
     def run_event(kind, what):
+        if kind == "z":
+            what()
+            return
         if kind == "w":
             for key in what.needs:
                 with jax.named_scope("w_" + "_".join(str(v) for v in key)):
@@ -362,19 +380,34 @@
     mark("first")
     while events[0][3] == "w" and events[0][0] < T0 + 0.1:
         run_event(*events.pop(0)[3:])
-    for m in (K, V, Q, O):
-        remote(w.at[m, mine], w.at[m, mine], zsend.at[m], zrecv.at[m], peer["zh"])
+    def swap_halves():
+        for m in (K, V, Q, O):
+            ref = w.at[m, mine]
+            remote(ref, ref, zsend.at[m], zrecv.at[m], peer["zh"], keep=False)
+
+    @pl.when(zh == 1)
+    def _():
+        pl.semaphore_signal(in_sem, inc=1, device_id=peer["zh"], device_id_type=MESH)
+        swap_halves()
+
+    for ch in range(TCH):
+        for d in (1, -1):
+            t_send(mp, ch, 1, d)
+
+    def answer():
+        @pl.when(zh == 0)
+        def _():
+            pl.semaphore_wait(in_sem, 1)
+            swap_halves()
+
+        for ch in range(TCH):
+            t_share(mp, ch)
+
+    events.append((T0 + 4.5, 2, 0, "z", answer))
+    events.sort(key=lambda e: e[:3])
     mark(None)
     now = T0
-    late_sends = 4
     while events or steps:
-        late_sends -= 1
-        if late_sends == 0:
-            for ch in range(TCH):
-                for d in (1, -1):
-                    t_send(mp, ch, 1, d)
-            for ch in range(TCH):
-                t_share(mp, ch)
         if events and (events[0][0] <= now or not steps):
             run_event(*events.pop(0)[3:])
         elif steps and steps[0][0] <= now:
@@ -404,15 +437,16 @@
         return jnp.where(z < nz // 2, t, nz - 1 - t)
 
     mark("outproj")
-    order = []
-    lo, hi = 0, nz - 1
-    while lo <= hi:
-        order += [hi, lo] if hi > lo else [lo]
-        lo, hi = lo + 1, hi - 1
-    for t in order:
+
+    def to_sibling(i, _):
+        t = jnp.where(lax.rem(i, 2) == 0, nz - 1 - i // 2, i // 2)
         zz = real(t)
         sib_out[zz] = out_block(zz, 1 - core).astype(BF16)
-        remote(sib_out.at[zz], sib_in.at[zz], psend.at[zz], precv.at[zz], sibling)
+        remote(sib_out.at[zz], sib_in.at[zz], psend.at[zz], precv.at[zz], sibling, keep=False)
+        return 0
+
+    lax.fori_loop(0, nz, to_sibling, 0)
+
     rr = rows // RCH
 
     def chunk(ch):
@@ -474,8 +508,11 @@
                     value = value + hop_in(t, ch, 1)
                     if uu > 0:
                         value = value + hop_in(t, ch, 0)
+                    attn_out[chunk(ch), :] = value
                     value = value + own_tok[chunk(ch), :].astype(F32)
-                    stream_out[chunk(ch), :] = value.astype(BF16)
+                    v = value.astype(BF16).astype(F32)
+                    total = jnp.broadcast_to(jnp.sum(v * v, axis=1, keepdims=True), (rr, 128))
+                    sq_in[mp, :, ch * rr : (ch + 1) * rr] = jnp.transpose(total)[0:8]
                     continue
                 if a == 1 or uu > 0:
                     value = value + hop_in(t, ch, a)
@@ -492,10 +529,6 @@
 
     mark("squares")
     half = 128
-    for r in range(rows // half):
-        v = stream_out[r * half : (r + 1) * half, :].astype(F32)
-        total = jnp.broadcast_to(jnp.sum(v * v, axis=1, keepdims=True), (half, 128))
-        sq_in[mp, :, r * half : (r + 1) * half] = jnp.transpose(total)[0:8]
     for k in range(1, n_mp):
         other = {"mp": lax.rem(mp + k, n_mp)}
         remote(sq_in.at[mp, pl.ds(0, 1)], sq_in.at[mp, pl.ds(0, 1)], qsend.at[k], qrecv.at[k], other)
@@ -511,9 +544,7 @@
         piece_t = jnp.transpose(
             jnp.broadcast_to(post[:, r * half : (r + 1) * half], (128, half))
         )
-        v = stream_out[r * half : (r + 1) * half, :].astype(F32)
-        scaled = v * piece_t[:, 0:1] * pgain_in[...].astype(F32).reshape(1, cols)
-        normed_out[r * half : (r + 1) * half, :] = scaled.astype(BF16)
+        scale_out[r * half : (r + 1) * half, :] = piece_t[:, 0:1] * pgain_in[...].astype(F32).reshape(1, cols)
 
     mark("drain")
     for c in sends:
@@ -533,6 +564,10 @@
                         device_id=sibling, device_id_type=MESH,
                     ).wait_send()
 
+    for m in (K, V, Q, O):
+        sent_off(w.at[m, mine], zsend.at[m], zrecv.at[m])
+    for zz in range(nz):
+        sent_off(sib_out.at[zz], psend.at[zz], precv.at[zz])
     for zz in range(nz):
         for ch in range(TCH):
             ref = t_slot(zz * NC + core, ch)
@@ -557,11 +592,11 @@
     any_spec = pl.BlockSpec(memory_space=pl.ANY)
     vmem = pl.BlockSpec(memory_space=pltpu.VMEM)
     dma = pltpu.SemaphoreType.DMA
-    return pl.pallas_call(
+    attention_out, scale = pl.pallas_call(
         functools.partial(body, nz),
         out_shape=(
-            jax.ShapeDtypeStruct((rows, cols), BF16),
-            jax.ShapeDtypeStruct((rows, cols), BF16),
+            jax.ShapeDtypeStruct((rows, cols), F32),
+            jax.ShapeDtypeStruct((rows, cols), F32),
         ),
         in_specs=[any_spec, vmem, any_spec, any_spec, any_spec, vmem],
         out_specs=(vmem, vmem),
@@ -579,6 +614,7 @@
             pltpu.VMEM((nz, rows, cols), BF16),
             pltpu.VMEM((n_mp, 8, rows), F32),
             dma((4,)),
+            pltpu.SemaphoreType.REGULAR,
             dma((n_msgs,)),
             dma((n_msgs,)),
             dma((4,)),
@@ -598,6 +634,9 @@
             collective_id=0, has_side_effects=True, vmem_limit_bytes=62 * 1024 * 1024
         ),
     )(tokens, pre_gain, input_weight, output_weight.T, position_bias, post_gain)
+    stream = lax.reduce_precision(tokens.astype(F32) + attention_out, 8, 7)
+    normed = (stream * scale).astype(BF16)
+    return stream.astype(BF16), normed
 
 
 def solution(mesh):

time: 123 us -> 111 us (0.902)
  Pallas kernels: 119 us -> 108 us
  local copies, waits for them, and re-layouts: 3.34 us -> 0.01 us
  other arithmetic: 0 us -> 2.09 us
    pallas_call x1, Pallas kernels: 119 us -> 108 us  [on_device(): pl.pallas_call(functools.partial(body, nz), out_shape=(jax.ShapeDtypeStru...]
    unnamed x2, local copies, waits for them, and re-layouts: 3.34 us -> 0.01 us
    convert_element_type x0 -> x1, other arithmetic: none -> 2.09 us  [on_device(): normed = (stream * scale).astype(BF16)]
where the time goes in v3:
time: 111 us
  Pallas kernels  108 us (97%)
  other arithmetic  2.09 us (2%)
    pallas_call x1, Pallas kernels, on_device(): pl.pallas_call(functools.partial(body, nz), out_shape=(jax.ShapeDtypeStru...  108 us

profile of v3, /device:TPU:1, one launch (start us, length us, event | category | flops | bytes accessed | tf_op | source)
XLA Modules:
  0.0 111.1 jit_solution(14904967505110186125)
XLA Ops:
  0.6 0.0 copy-start
  0.6 108.3 %shard_map.77 = (f32[512,256]{1,0:T(8,128)}, f32[512,256]{1,0:T(8,128)}) custom-call(bf16[512,256]{1,0:T(8,128)(2,1)} %tok_in.1, bf16[256]{0:T(256)(128)(2,1)} %gain_in.1, bf16[3,48,256]{2,1,0:T(8,128)(2,1)} %wi_in.1, bf16[48,256]{1,0:T(8,128)(2,1)} %bitcast.1, bf16[4,512,512]{2,1,0:T(8,128)(2,1)} %bias_in.1, bf16[256]{0:T(256)(128)(2,1)} %pgain_in.1), custom_call_target="tpu_custom_call" | custom-call | tf_op jit(solution)/shard_map/pallas_call | solution.py:595
  109.0 0.0 copy-done
  109.0 2.1 %multiply_convert_fusion = (bf16[512,256]{1,0:T(8,128)(2,1)}, bf16[512,256]{1,0:T(8,128)(2,1)}) fusion(f32[512,256]{1,0:T(8,128)} %get-tuple-element.5, f32[512,256]{1,0:T(8,128)} %get-tuple-element.4, bf16[512,256]{1,0:T(8,128)(2,1)S(1)} %copy-done), kind=kLoop, calls=%fused_computation | loop fusion | flops 786432 | bytes 1835008 | tf_op jit(solution)/shard_map/convert_element_type | solution.py:638
Async XLA Ops:
  0.6 108.3 %copy-start = (bf16[512,256]{1,0:T(8,128)(2,1)S(1)}, bf16[512,256]{1,0:T(8,128)(2,1)}, u32[]{:S(2)}) copy-start(bf16[512,256]{1,0:T(8,128)(2,1)} %tok_in.1) | copy-start | bytes 786436

commit v4 on v3

--- a/solution.py
+++ b/solution.py
@@ -15,9 +15,12 @@
 NH, NY, NX = 2, 8, 4
 NC = 2
 Q, K, V, O = 0, 1, 2, 3
-XY_MATS = (Q, O)
+OA, OB = 3, 4
+MAT = (Q, K, V, O, O)
+LATE = (OA, OB)
+XY_STREAMS = (Q, OA)
 SPLIT = 2
-TCH = 2
+TCH = 4
 RCH = 4
 LATE_START = 0.0
 FIRST_LATE = 2.5
@@ -52,21 +55,22 @@
         return got
 
     for half in (0, 1):
-        for m in (K, V, Q, O):
+        for m in (K, V, Q, OA, OB):
+            unit = 0.5 if m in LATE else 1
             own = [("own", m, half)]
             parity = m + half
-            if m in XY_MATS:
-                got = ring((m, half, "X", 0), "x", NX, 1, own, parity)
+            if m in XY_STREAMS:
+                got = ring((m, half, "X", 0), "x", NX, unit, own, parity)
                 near = got[0] + got[1] + got[-1]
                 far = near + got[NX // 2]
                 for g in range(SPLIT):
                     needs = near if g == 0 and SPLIT > 1 else far
-                    ring((m, half, "Y", g), "y", NY, NX // SPLIT, needs, parity + g)
+                    ring((m, half, "Y", g), "y", NY, unit * NX // SPLIT, needs, parity + g)
             else:
-                got = ring((m, half, "Y", 0), "y", NY, 1, own, parity)
+                got = ring((m, half, "Y", 0), "y", NY, unit, own, parity)
                 order = sorted(got, key=lambda b: (abs(b), b))
                 for g, b in enumerate(order):
-                    ring((m, half, "X", b), "x", NX, 1, got[b], parity + g)
+                    ring((m, half, "X", b), "x", NX, unit, got[b], parity + g)
     return msgs
 
 
@@ -87,7 +91,7 @@
             if all(n in avail for n in msg.needs):
                 ready = max(avail[n] for n in msg.needs)
                 rank = -tail.get(msg.key, 0.0)
-                if msg.key[0] == O:
+                if msg.key[0] in LATE:
                     rank += LATE_RANK
                     if msg.key[2] == "Y":
                         ready = max(ready, LATE_START)
@@ -106,7 +110,7 @@
 
 def body(
     nz, tok_in, gain_in, wi_in, wo_in, bias_in, pgain_in, attn_out, scale_out,
-    tok, w, bias, xn, qkv, ctx, pown, sib_out, sib_in, rin, sout, sq_in,
+    tok, w, bias, xn, ss, acc, qkv, ctx, pown, sib_out, sib_in, rin, sout, sq_in,
     loc_sem, in_sem, wsend, wrecv, zsend, zrecv, tsend, trecv, bsend, brecv,
     psend, precv, rsend, rrecv, qsend, qrecv,
 ):
@@ -178,20 +182,17 @@
     for g in range(cols // min(128, cols)):
         half_l = min(128, cols)
         qkv[V, g, :, half_l:] = jnp.ones((rows, half_l), BF16)
-        ctx[g] = jnp.zeros((rows, half_l), BF16)
+    ss[...] = jnp.zeros_like(ss)
+    for m in range(3):
+        acc[m] = jnp.zeros((rows, cols), F32)
     pl.semaphore_wait(barrier, len(peer) - 1 + n_mp - 1 + zh)
 
-    sends = []
-
-    def remote(src, dst, ssem, rsem, device, keep=True):
+    def remote(src, dst, ssem, rsem, device):
         c = pltpu.make_async_remote_copy(
             src_ref=src, dst_ref=dst, send_sem=ssem, recv_sem=rsem,
             device_id=device, device_id_type=MESH,
         )
         c.start()
-        if keep:
-            sends.append(c)
-        return c
 
     def arrival(ref, ssem, rsem):
         pltpu.make_async_remote_copy(
@@ -209,7 +210,7 @@
         m, half, kind, g, s, d = msg.key
         h = zh if half == 0 else 1 - zh
         hop = d * (msg.step - 1 + back)
-        if m in XY_MATS:
+        if m in XY_STREAMS:
             if kind == "X":
                 row, n = dp_of(h, y, wrap(x - hop, NX)), 1
             else:
@@ -222,7 +223,10 @@
                 row = dp_of(h, wrap(y - hop, NY), x)
             else:
                 row = dp_of(h, wrap(y + g, NY), wrap(x - hop, NX))
-        return w.at[m, pl.ds(pl.multiple_of(row * blk, 16), n * blk)]
+        at = pl.ds(pl.multiple_of(row * blk, 16), n * blk)
+        if m in LATE:
+            return w.at[MAT[m], at, pl.ds((m - OA) * (cols // 2), cols // 2)]
+        return w.at[m, at]
 
     crow = rows // TCH
 
@@ -232,18 +236,27 @@
 
     T0 = 1.5
     arrivals = {}
-    for m in (Q, K, V, O):
+    for m in range(len(MAT)):
         arrivals["own", m, 0] = T0
-    for i, m in enumerate((K, V, Q, O)):
+    for i, m in enumerate((K, V, Q, OA, OB)):
         arrivals["own", m, 1] = T0 + 9.5 + 0.7 * i
     schedule, when_in = weight_schedule(arrivals)
-    index = {msg.key: i for i, (_, msg) in enumerate(schedule)}
     by_key = {msg.key: msg for _, msg in schedule}
+    passed_on = {n for msg in by_key.values() for n in msg.needs}
+    leaf_rows = [0] * len(MAT)
+    slot_of = {}
+    for key, msg in by_key.items():
+        if key in passed_on:
+            slot_of[key] = len(MAT) + len(slot_of)
+        else:
+            leaf_rows[key[0]] += int(msg.size * (2 if key[0] in LATE else 1)) * blk
+    for key in by_key:
+        slot_of.setdefault(key, key[0])
     in_order = sorted(by_key, key=lambda k: when_in[k])
     events = [(t, 1, i, "w", msg) for i, (t, msg) in enumerate(schedule)]
     for s in range(1, nz):
         for ch in range(TCH):
-            t = 13.0 + 5.8 * (s - 1) + 2.9 * ch if s > 1 else 9.0 + 2.9 * ch
+            t = 10.5 + 5.8 * (s - 1) + 5.8 * ch / TCH
             events.append((t, 0, s * TCH + ch, "t", (s, ch)))
     t_tokens = max(e[0] for e in events if e[3] == "t") + 1.5
     events.sort(key=lambda e: e[:3])
@@ -255,24 +268,35 @@
             return
         waited.add(key)
         if key[0] == "own":
-            m = key[1]
+            m = MAT[key[1]]
+            if ("own", m) in waited:
+                return
+            waited.add(("own", m))
             there = pl.ds(pl.multiple_of(dp_of(1 - zh, y, x) * blk, 16), blk)
-            arrival(w.at[m, there], zsend.at[m], zrecv.at[m])
+            arrival(w.at[m, there], zsend.at[0], zrecv.at[m])
         else:
-            i = index[key]
-            arrival(w_slot(by_key[key], 1), wsend.at[i], wrecv.at[i])
+            i = slot_of[key]
+            if i >= len(MAT):
+                arrival(w_slot(by_key[key], 1), wsend.at[0], wrecv.at[i])
+            elif ("leaves", i) not in waited:
+                waited.add(("leaves", i))
+                some = pl.ds(0, leaf_rows[i])
+                if i in LATE:
+                    ref = w.at[MAT[i], some, pl.ds(0, cols // 2)]
+                else:
+                    ref = w.at[i, some]
+                arrival(ref, wsend.at[0], wrecv.at[i])
 
     def t_send(owner, ch, s, d):
         @pl.when((z + d >= 0) & (z + d < nz))
         def _():
             ref = t_slot(owner, ch)
             i = ((s - 1) * TCH + ch) * 2 + (d > 0)
-            remote(ref, ref, tsend.at[i], trecv.at[i], {"mp": mp + d * NC}, keep=False)
+            remote(ref, ref, tsend.at[(s - 1) * 2 + (d > 0)], trecv.at[i], {"mp": mp + d * NC})
 
     def t_share(owner, ch):
         ref = t_slot(owner, ch)
-        i = owner // NC * TCH + ch
-        remote(ref, ref, bsend.at[i], brecv.at[i], sibling, keep=False)
+        remote(ref, ref, bsend.at[0], brecv.at[owner // NC], sibling)
 
     def run_event(kind, what):
         if kind == "z":
@@ -282,9 +306,9 @@
             for key in what.needs:
                 with jax.named_scope("w_" + "_".join(str(v) for v in key)):
                     wait_w(key)
-            i = index[what.key]
+            i = slot_of[what.key]
             ref = w_slot(what, 0)
-            remote(ref, ref, wsend.at[i], wrecv.at[i], peer[what.link])
+            remote(ref, ref, wsend.at[0], wrecv.at[i], peer[what.link])
             return
         s, ch = what
         for d in (1, -1):
@@ -294,47 +318,69 @@
                 owner = mp - d * s * NC
                 i = ((s - 1) * TCH + ch) * 2 + (d > 0)
                 with jax.named_scope("t_%d_%d_%d" % (s, ch, d)):
-                    arrival(t_slot(owner, ch), tsend.at[i], trecv.at[i])
+                    arrival(t_slot(owner, ch), tsend.at[0], trecv.at[i])
                 if s + 1 < nz:
                     t_send(owner, ch, s + 1, d)
                 t_share(owner, ch)
 
     d_model = n_mp * cols
     step = min(64, rows)
-    part = min(512, rows)
-    n_part = rows // part
-
-    def tokens_done():
-        for zz in range(nz):
-            for ch in range(TCH):
-                owner = zz * NC + 1 - core
-                i = zz * TCH + ch
-                arrival(t_slot(owner, ch), bsend.at[i], brecv.at[i])
-
-    def norm_rows(r, _):
-        at = pl.ds(pl.multiple_of(r * step, step), step)
-        acc = jnp.zeros((step, cols), F32)
-        for i in range(n_mp):
-            v = tok[i, at, :].astype(F32)
-            acc += v * v
-        inv = lax.rsqrt(jnp.sum(acc, axis=1, keepdims=True) / d_model + EPS)
-        for i in range(n_mp):
-            gain = tok[i, pl.ds(rows, GAIN_ROWS), :].astype(F32)[0:1]
-            v = tok[i, at, :].astype(F32)
-            xn[at, i * cols : (i + 1) * cols] = (v * inv * gain).astype(BF16)
-        return 0
-
-    def norm_part(p):
-        per = 128 // step
-        lax.fori_loop(p * per, (p + 1) * per, norm_rows, 0)
-
-    def project():
+    half_rows = rows // 2
+
+    def widen(zz):
+        arrival(tok.at[zz * NC + 1 - core], bsend.at[0], brecv.at[zz])
+
+        def some(r, _):
+            at = pl.ds(pl.multiple_of(r * step, step), step)
+            total = ss[at, :]
+            for c in range(NC):
+                gain = tok[zz * NC + c, pl.ds(rows, GAIN_ROWS), :].astype(F32)[0:1]
+                v = tok[zz * NC + c, at, :].astype(F32)
+                total += v * v
+                xn[zz, at, c * cols : (c + 1) * cols] = (v * gain).astype(BF16)
+            ss[at, :] = total
+            return 0
+
+        lax.fori_loop(0, rows // step, some, 0)
+
+    def absorb(m, zz):
+        here = pl.ds(pl.multiple_of(zz * NC * cols, NC * cols), NC * cols)
+        acc[m] += jnp.dot(xn[zz], w[m, here, :], preferred_element_type=F32)
+
+    def each_far(lo, hi, call):
+        def one(zz, _):
+            far = jnp.abs(zz - z)
+
+            @pl.when((far >= lo) & (far <= hi))
+            def _():
+                call(zz)
+
+            return 0
+
+        lax.fori_loop(0, nz, one, 0)
+
+    def absorb_all(zz):
+        def one(m, _):
+            absorb(m, zz)
+            return 0
+
+        lax.fori_loop(0, 3, one, 0)
+
+    def absorb_near(m, hi):
         for key in in_order:
-            if key[0] != O:
+            if key[0] == m:
                 wait_w(key)
+        each_far(0, hi, functools.partial(absorb, m))
+
+    def late_block(s):
+        each_far(s, s, widen)
+        each_far(s, s, absorb_all)
+
+    def projected():
+        inv = lax.rsqrt(jnp.sum(ss[...], axis=1, keepdims=True) / d_model + EPS)
 
         def one(m, _):
-            r = jnp.dot(xn[...], w[m], preferred_element_type=F32).astype(BF16)
+            r = (acc[m] * inv).astype(BF16)
             for g in range(groups):
                 qkv[m, g, :, 0:lanes] = r[:, g * lanes : (g + 1) * lanes]
             return 0
@@ -345,37 +391,47 @@
     groups = cols // lanes
     per = lanes // hd
 
-    def attend_one(i, _):
-        h = lax.rem(i, heads)
-        at = pl.ds(pl.multiple_of(i // heads * part, part), part)
-        g = h // per
-        first = lax.rem(h, per) * hd
-        lane = lax.broadcasted_iota(jnp.int32, (part, lanes), 1)
-        mine_l = (lane >= first) & (lane < first + hd)
-        q = jnp.where(mine_l, qkv[Q, g, at, 0:lanes], jnp.zeros((), BF16))
-        s = lax.dot_general(
-            q, qkv[K, g, :, 0:lanes],
-            (((1,), (1,)), ((), ())), preferred_element_type=F32,
-        )
-        s = s + bias[h, at, :].astype(F32)
-        e = jnp.exp(s - jnp.max(s, axis=1, keepdims=True)).astype(BF16)
-        o = jnp.dot(e, qkv[V, g], preferred_element_type=F32)
-        o = (o[:, 0:lanes] * (1.0 / o[:, lanes:])).astype(BF16)
-        ctx[g, at, :] = jnp.where(mine_l, o, ctx[g, at, :])
-        return 0
-
-    def attend(i):
-        lax.fori_loop(2 * i, 2 * i + 2, attend_one, 0)
-
-    t_of = {m: max(when_in[k] for k in in_order if k[0] == m) for m in (Q, K, V)}
-    t_proj = max(list(t_of.values()) + [t_tokens])
-    steps = [(t_tokens, 0.02, "tokens", tokens_done)]
-    for p in range(rows // 128):
-        steps.append((t_tokens, 0.37, "norm_in", functools.partial(norm_part, p)))
-    steps.append((t_proj, 2.9, "project", project))
-    steps.append((t_proj, 0.0, "bias", copies[3].wait))
-    for i in range(n_part * heads // 2):
-        steps.append((t_proj, 1.6, "attend", functools.partial(attend, i)))
+    def attend(p):
+        at = pl.ds(p * half_rows, half_rows)
+        lane = lax.broadcasted_iota(jnp.int32, (half_rows, lanes), 1)
+
+        def one(g, _):
+            both = jnp.zeros((half_rows, lanes), F32)
+            for j in range(per):
+                mine_l = (lane >= j * hd) & (lane < (j + 1) * hd)
+                q = jnp.where(mine_l, qkv[Q, g, at, 0:lanes], jnp.zeros((), BF16))
+                s = lax.dot_general(
+                    q, qkv[K, g, :, 0:lanes],
+                    (((1,), (1,)), ((), ())), preferred_element_type=F32,
+                )
+                s = s + bias[g * per + j, at, :].astype(F32)
+                e = jnp.exp(s - jnp.max(s, axis=1, keepdims=True)).astype(BF16)
+                o = jnp.dot(e, qkv[V, g], preferred_element_type=F32)
+                both = jnp.where(mine_l, o[:, 0:lanes] * (1.0 / o[:, lanes:]), both)
+            ctx[g, at, :] = both.astype(BF16)
+            return 0
+
+        lax.fori_loop(0, groups, one, 0)
+
+    t_all = max(when_in[k] for k in in_order if k[0] not in LATE)
+    t_w = {K: t_all - 1.8, Q: t_all - 0.7, V: t_all + 1.0}
+    t_tok = {0: 8.0}
+    for e in events:
+        if e[3] == "t":
+            t_tok[e[4][0]] = max(t_tok.get(e[4][0], 0.0), e[0] + 2.0)
+    early = max([s for s in range(nz) if t_tok[s] < min(t_w.values())])
+    steps = []
+    for s in range(early + 1):
+        call = functools.partial(each_far, s, s, widen)
+        steps.append((t_tok[s] + 5.0, 0.4, "widen_%d" % s, call))
+    for m in (K, V, Q):
+        call = functools.partial(absorb_near, m, early)
+        steps.append((t_w[m], 1.2, "absorb_m%d" % m, call))
+    steps.sort(key=lambda e: e[0])
+    for s in range(early + 1, nz):
+        call = functools.partial(late_block, s)
+        steps.append((max(t_tok[s], t_all + 2.5), 1.1, "absorb_%d" % s, call))
+    steps.append((t_tok[nz - 1], 0.4, "projected", projected))
 
     mark("first")
     while events[0][3] == "w" and events[0][0] < T0 + 0.1:
@@ -383,7 +439,7 @@
     def swap_halves():
         for m in (K, V, Q, O):
             ref = w.at[m, mine]
-            remote(ref, ref, zsend.at[m], zrecv.at[m], peer["zh"], keep=False)
+            remote(ref, ref, zsend.at[0], zrecv.at[m], peer["zh"])
 
     @pl.when(zh == 1)
     def _():
@@ -418,13 +474,17 @@
         else:
             now = min(e[0][0] for e in (events, steps) if e)
 
+    mark("attend")
+    copies[3].wait()
+    attend(0)
     mark("owait")
     for key in in_order:
         wait_w(key)
 
-    def out_block(zz, c):
+    def out_block(zz, c, p):
         at = pl.ds(pl.multiple_of((zz * NC + c) * cols, cols), cols)
-        whole = jnp.concatenate([ctx[g] for g in range(groups)], axis=1)
+        rp = pl.ds(p * half_rows, half_rows)
+        whole = jnp.concatenate([ctx[g, rp, :] for g in range(groups)], axis=1)
         return lax.dot_general(
             whole, w[O, at, :], (((1,), (1,)), ((), ())), preferred_element_type=F32
         )
@@ -438,14 +498,21 @@
 
     mark("outproj")
 
-    def to_sibling(i, _):
+    def sib_part(ref, zz, p):
+        return ref.at[zz, pl.ds(p * half_rows, half_rows)]
+
+    def to_sibling(p, i, _):
         t = jnp.where(lax.rem(i, 2) == 0, nz - 1 - i // 2, i // 2)
         zz = real(t)
-        sib_out[zz] = out_block(zz, 1 - core).astype(BF16)
-        remote(sib_out.at[zz], sib_in.at[zz], psend.at[zz], precv.at[zz], sibling, keep=False)
+        j = zz * 2 + p
+        sib_out[zz, pl.ds(p * half_rows, half_rows), :] = out_block(zz, 1 - core, p).astype(BF16)
+        remote(
+            sib_part(sib_out, zz, p), sib_part(sib_in, zz, p),
+            psend.at[0], precv.at[j], sibling,
+        )
         return 0
 
-    lax.fori_loop(0, nz, to_sibling, 0)
+    lax.fori_loop(0, nz, functools.partial(to_sibling, 0), 0)
 
     rr = rows // RCH
 
@@ -456,17 +523,18 @@
 
     def pair_sum(t, ch, uu):
         zz = real(t)
-        if (uu, t) not in joined:
-            joined.add((uu, t))
-            pown[zz] = out_block(zz, core)
-            arrival(sib_in.at[zz], psend.at[zz], precv.at[zz])
+        p = ch * 2 // RCH
+        if (uu, t, p) not in joined:
+            joined.add((uu, t, p))
+            pown[zz, pl.ds(p * half_rows, half_rows), :] = out_block(zz, core, p)
+            arrival(sib_part(sib_in, zz, p), psend.at[0], precv.at[zz * 2 + p])
         return pown[zz, chunk(ch), :] + sib_in[zz, chunk(ch), :].astype(F32)
 
     def hop_in(t, ch, a):
         zz = real(t)
         way = near if a == 0 else 1 - near
         i = (way * nz + zz) * RCH + ch
-        arrival(rin.at[way, zz, chunk(ch)], rsend.at[i], rrecv.at[i])
+        arrival(rin.at[way, zz, chunk(ch)], rsend.at[0], rrecv.at[i])
         return rin[way, zz, chunk(ch), :].astype(F32)
 
     def hop_out(t, ch, a, value):
@@ -477,10 +545,20 @@
         to = mp + NC * (sigma if a == 0 else -sigma)
         remote(
             sout.at[zz, chunk(ch)], rin.at[way, zz, chunk(ch)],
-            rsend.at[i], rrecv.at[i], {"mp": to}, keep=False,
+            rsend.at[0], rrecv.at[i], {"mp": to},
         )
 
     mark("reduce")
+    @pl.when(u == 0)
+    def _():
+        for ch in range(RCH // 2):
+            hop_out(nz - 1, ch, 0, pair_sum(nz - 1, ch, 0))
+
+    mark("attend2")
+    attend(1)
+    lax.fori_loop(0, nz, functools.partial(to_sibling, 1), 0)
+    mark("reduce")
+
     hop, piece = 3.8, 5.6
     own_tok = tok.at[mp]
     for uu in range(nz // 2):
@@ -503,6 +581,8 @@
                     at = max(at, (nz - uu) * piece + hop + ch * piece / RCH)
                 moves.append((at, 2, uu, ch))
             for _, a, t, ch in sorted(moves):
+                if uu == 0 and a == 0 and t == nz - 1 and ch < RCH // 2:
+                    continue
                 value = pair_sum(t, ch, uu)
                 if a == 2:
                     value = value + hop_in(t, ch, 1)
@@ -517,24 +597,14 @@
                 if a == 1 or uu > 0:
                     value = value + hop_in(t, ch, a)
                 hop_out(t, ch, a, value)
-            for _, a, t, ch in sorted(todo):
-                zz = real(t)
-                way = near if a == 0 else 1 - near
-                i = (way * nz + zz) * RCH + ch
-                pltpu.make_async_remote_copy(
-                    src_ref=sout.at[zz, chunk(ch)], dst_ref=sout.at[zz, chunk(ch)],
-                    send_sem=rsend.at[i], recv_sem=rrecv.at[i],
-                    device_id=sibling, device_id_type=MESH,
-                ).wait_send()
 
     mark("squares")
     half = 128
     for k in range(1, n_mp):
         other = {"mp": lax.rem(mp + k, n_mp)}
-        remote(sq_in.at[mp, pl.ds(0, 1)], sq_in.at[mp, pl.ds(0, 1)], qsend.at[k], qrecv.at[k], other)
-    for k in range(1, n_mp):
-        source = lax.rem(mp + n_mp - k, n_mp)
-        arrival(sq_in.at[source, pl.ds(0, 1)], qsend.at[k], qrecv.at[k])
+        remote(sq_in.at[mp, pl.ds(0, 1)], sq_in.at[mp, pl.ds(0, 1)], qsend.at[0], qrecv.at[0], other)
+    others = sq_in.at[pl.ds(0, n_mp - 1), pl.ds(0, 1)]
+    arrival(others, qsend.at[0], qrecv.at[0])
     mark("final")
     total = sq_in[0, 0:1, :]
     for i in range(1, n_mp):
@@ -547,36 +617,22 @@
         scale_out[r * half : (r + 1) * half, :] = piece_t[:, 0:1] * pgain_in[...].astype(F32).reshape(1, cols)
 
     mark("drain")
-    for c in sends:
-        c.wait_send()
+    w_rows = int(sum(msg.size for msg in by_key.values())) * blk // 4
+    sent_off(w.at[:, pl.ds(0, w_rows)], wsend.at[0], wrecv.at[0])
     for s in range(1, nz):
-        for ch in range(TCH):
-            for d in (1, -1):
-                sent = (z + d >= 0) & (z + d < nz)
-                held = (z - d * (s - 1) >= 0) & (z - d * (s - 1) < nz)
-
-                @pl.when(sent & held)
-                def _():
-                    ref = t_slot(mp, ch)
-                    i = ((s - 1) * TCH + ch) * 2 + (d > 0)
-                    pltpu.make_async_remote_copy(
-                        src_ref=ref, dst_ref=ref, send_sem=tsend.at[i], recv_sem=trecv.at[i],
-                        device_id=sibling, device_id_type=MESH,
-                    ).wait_send()
-
-    for m in (K, V, Q, O):
-        sent_off(w.at[m, mine], zsend.at[m], zrecv.at[m])
-    for zz in range(nz):
-        sent_off(sib_out.at[zz], psend.at[zz], precv.at[zz])
-    for zz in range(nz):
-        for ch in range(TCH):
-            ref = t_slot(zz * NC + core, ch)
-            i = zz * TCH + ch
-            pltpu.make_async_remote_copy(
-                src_ref=ref, dst_ref=ref, send_sem=bsend.at[i], recv_sem=brecv.at[i],
-                device_id=sibling, device_id_type=MESH,
-            ).wait_send()
-
+        for d in (1, -1):
+            sent = (z + d >= 0) & (z + d < nz)
+            held = (z - d * (s - 1) >= 0) & (z - d * (s - 1) < nz)
+
+            @pl.when(sent & held)
+            def _(s=s, d=d):
+                sent_off(tok.at[mp], tsend.at[(s - 1) * 2 + (d > 0)], trecv.at[0])
+
+    sent_off(w.at[:, mine], zsend.at[0], zrecv.at[0])
+    sent_off(tok.at[pl.ds(0, nz)], bsend.at[0], brecv.at[0])
+    sent_off(sib_out, psend.at[0], precv.at[0])
+    sent_off(sout.at[pl.ds(0, nz - 1)], rsend.at[0], rrecv.at[0])
+    sent_off(others, qsend.at[0], qrecv.at[0])
     mark(None)
 
 
@@ -587,7 +643,9 @@
     n_dp = lax.axis_size("dp")
     nz = n_mp // NC
     heads, seq, _ = position_bias.shape
-    n_msgs = len(weight_messages())
+    msgs = weight_messages()
+    passed_on = {n for msg in msgs for n in msg.needs}
+    n_slots = len(MAT) + sum(msg.key in passed_on for msg in msgs)
     lanes = min(128, cols)
     any_spec = pl.BlockSpec(memory_space=pl.ANY)
     vmem = pl.BlockSpec(memory_space=pltpu.VMEM)
@@ -604,7 +662,9 @@
             pltpu.VMEM((n_mp, rows + GAIN_ROWS, cols), BF16),
             pltpu.VMEM((4, n_dp * blk, cols), BF16),
             pltpu.VMEM((heads, seq, seq), BF16),
-            pltpu.VMEM((rows, n_mp * cols), BF16),
+            pltpu.VMEM((nz, rows, NC * cols), BF16),
+            pltpu.VMEM((rows, cols), F32),
+            pltpu.VMEM((3, rows, cols), F32),
             pltpu.VMEM((3, cols // lanes, rows, 2 * lanes), BF16),
             pltpu.VMEM((cols // lanes, rows, lanes), BF16),
             pltpu.VMEM((nz, rows, cols), F32),
@@ -615,20 +675,20 @@
             pltpu.VMEM((n_mp, 8, rows), F32),
             dma((4,)),
             pltpu.SemaphoreType.REGULAR,
-            dma((n_msgs,)),
-            dma((n_msgs,)),
+            dma((1,)),
+            dma((n_slots,)),
+            dma((1,)),
             dma((4,)),
-            dma((4,)),
+            dma((2 * (nz - 1),)),
             dma((2 * TCH * (nz - 1),)),
-            dma((2 * TCH * (nz - 1),)),
-            dma((nz * TCH,)),
-            dma((nz * TCH,)),
+            dma((1,)),
             dma((nz,)),
-            dma((nz,)),
+            dma((1,)),
+            dma((2 * nz,)),
+            dma((1,)),
             dma((2 * nz * RCH,)),
-            dma((2 * nz * RCH,)),
-            dma((n_mp,)),
-            dma((n_mp,)),
+            dma((1,)),
+            dma((1,)),
         ],
         compiler_params=pltpu.CompilerParams(
             collective_id=0, has_side_effects=True, vmem_limit_bytes=62 * 1024 * 1024

time: 111 us -> 104 us (0.937)
  Pallas kernels: 108 us -> 101 us
    pallas_call x1, Pallas kernels: 108 us -> 101 us  [on_device(): pl.pallas_call(functools.partial(body, nz), out_shape=(jax.ShapeDtypeStru...]
where the time goes in v4:
time: 104 us; the launch traced here: 103 us
  Pallas kernels  101 us (97%)
  other arithmetic  2.09 us (2%)
    pallas_call x1, Pallas kernels, on_device(): pl.pallas_call(functools.partial(body, nz), out_shape=(jax.ShapeDtypeStru...  101 us
    convert_element_type x1, other arithmetic, on_device(): normed = (stream * scale).astype(BF16)  2.09 us

profile of v4, /device:TPU:1, one launch (start us, length us, event | category | flops | bytes accessed | tf_op | source)
XLA Modules:
  0.0 103.5 jit_solution(12828597376876819886)
XLA Ops:
  0.6 0.0 copy-start
  0.6 100.7 %shard_map.77 = (f32[512,256]{1,0:T(8,128)}, f32[512,256]{1,0:T(8,128)}) custom-call(bf16[512,256]{1,0:T(8,128)(2,1)} %tok_in.1, bf16[256]{0:T(256)(128)(2,1)} %gain_in.1, bf16[3,48,256]{2,1,0:T(8,128)(2,1)} %wi_in.1, bf16[48,256]{1,0:T(8,128)(2,1)} %bitcast.1, bf16[4,512,512]{2,1,0:T(8,128)(2,1)} %bias_in.1, bf16[256]{0:T(256)(128)(2,1)} %pgain_in.1), custom_call_target="tpu_custom_call" | custom-call | tf_op jit(solution)/shard_map/pallas_call | solution.py:653
  101.4 0.0 copy-done
  101.4 2.1 %multiply_convert_fusion = (bf16[512,256]{1,0:T(8,128)(2,1)}, bf16[512,256]{1,0:T(8,128)(2,1)}) fusion(f32[512,256]{1,0:T(8,128)} %get-tuple-element.5, f32[512,256]{1,0:T(8,128)} %get-tuple-element.4, bf16[512,256]{1,0:T(8,128)(2,1)S(1)} %copy-done), kind=kLoop, calls=%fused_computation | loop fusion | flops 786432 | bytes 1835008 | tf_op jit(solution)/shard_map/convert_element_type | solution.py:698
Async XLA Ops:
  0.6 100.7 %copy-start = (bf16[512,256]{1,0:T(8,128)(2,1)S(1)}, bf16[512,256]{1,0:T(8,128)(2,1)}, u32[]{:S(2)}) copy-start(bf16[512,256]{1,0:T(8,128)(2,1)} %tok_in.1) | copy-start | bytes 786436

commit v5 on v4

--- a/solution.py
+++ b/solution.py
@@ -15,8 +15,9 @@
 NH, NY, NX = 2, 8, 4
 NC = 2
 Q, K, V, O = 0, 1, 2, 3
-OA, OB = 3, 4
-MAT = (Q, K, V, O, O)
+KV, OA, OB = 1, 2, 3
+MAT = (Q, K, O, O)
+STREAM = (Q, KV, KV)
 LATE = (OA, OB)
 XY_STREAMS = (Q, OA)
 SPLIT = 2
@@ -55,8 +56,8 @@
         return got
 
     for half in (0, 1):
-        for m in (K, V, Q, OA, OB):
-            unit = 0.5 if m in LATE else 1
+        for m in (KV, Q, OA, OB):
+            unit = 0.5 if m in LATE else 2 if m == KV else 1
             own = [("own", m, half)]
             parity = m + half
             if m in XY_STREAMS:
@@ -110,7 +111,7 @@
 
 def body(
     nz, tok_in, gain_in, wi_in, wo_in, bias_in, pgain_in, attn_out, scale_out,
-    tok, w, bias, xn, ss, acc, qkv, ctx, pown, sib_out, sib_in, rin, sout, sq_in,
+    gain_v, pgain_v, tok, w, bias, xn, ss, acc, qkv, ctx, pown, sib_out, sib_in, rin, sout, sq_in,
     loc_sem, in_sem, wsend, wrecv, zsend, zrecv, tsend, trecv, bsend, brecv,
     psend, precv, rsend, rrecv, qsend, qrecv,
 ):
@@ -158,7 +159,9 @@
         pltpu.make_async_copy(wo_in, w.at[O, mine], loc_sem.at[2]),
         pltpu.make_async_copy(bias_in, bias, loc_sem.at[3]),
     ]
-    for c in copies:
+    gain_copy = pltpu.make_async_copy(gain_in, gain_v, loc_sem.at[4])
+    pgain_copy = pltpu.make_async_copy(pgain_in, pgain_v, loc_sem.at[5])
+    for c in [gain_copy] + copies[:3]:
         c.start()
 
     barrier = pltpu.get_barrier_semaphore()
@@ -173,18 +176,14 @@
     for k in range(1, n_mp):
         other = {"mp": lax.rem(mp + k, n_mp)}
         pl.semaphore_signal(barrier, inc=1, device_id=other, device_id_type=MESH)
+
+    gain_copy.wait()
     tok[mp, rows : rows + GAIN_ROWS, :] = jnp.broadcast_to(
-        gain_in[...].astype(F32).reshape(1, cols), (GAIN_ROWS, cols)
+        gain_v[...].astype(F32).reshape(1, cols), (GAIN_ROWS, cols)
     ).astype(BF16)
     copies[2].wait()
     copies[0].wait()
     copies[1].wait()
-    for g in range(cols // min(128, cols)):
-        half_l = min(128, cols)
-        qkv[V, g, :, half_l:] = jnp.ones((rows, half_l), BF16)
-    ss[...] = jnp.zeros_like(ss)
-    for m in range(3):
-        acc[m] = jnp.zeros((rows, cols), F32)
     pl.semaphore_wait(barrier, len(peer) - 1 + n_mp - 1 + zh)
 
     def remote(src, dst, ssem, rsem, device):
@@ -226,7 +225,9 @@
         at = pl.ds(pl.multiple_of(row * blk, 16), n * blk)
         if m in LATE:
             return w.at[MAT[m], at, pl.ds((m - OA) * (cols // 2), cols // 2)]
-        return w.at[m, at]
+        if m == KV:
+            return w.at[pl.ds(K, 2), at]
+        return w.at[MAT[m], at]
 
     crow = rows // TCH
 
@@ -238,7 +239,7 @@
     arrivals = {}
     for m in range(len(MAT)):
         arrivals["own", m, 0] = T0
-    for i, m in enumerate((K, V, Q, OA, OB)):
+    for i, m in enumerate((KV, Q, OA, OB)):
         arrivals["own", m, 1] = T0 + 9.5 + 0.7 * i
     schedule, when_in = weight_schedule(arrivals)
     by_key = {msg.key: msg for _, msg in schedule}
@@ -249,7 +250,7 @@
         if key in passed_on:
             slot_of[key] = len(MAT) + len(slot_of)
         else:
-            leaf_rows[key[0]] += int(msg.size * (2 if key[0] in LATE else 1)) * blk
+            leaf_rows[key[0]] += int(msg.size * (2 if key[0] in LATE else 0.5 if key[0] == KV else 1)) * blk
     for key in by_key:
         slot_of.setdefault(key, key[0])
     in_order = sorted(by_key, key=lambda k: when_in[k])
@@ -274,6 +275,8 @@
             waited.add(("own", m))
             there = pl.ds(pl.multiple_of(dp_of(1 - zh, y, x) * blk, 16), blk)
             arrival(w.at[m, there], zsend.at[0], zrecv.at[m])
+            if m == K:
+                arrival(w.at[V, there], zsend.at[0], zrecv.at[V])
         else:
             i = slot_of[key]
             if i >= len(MAT):
@@ -283,8 +286,10 @@
                 some = pl.ds(0, leaf_rows[i])
                 if i in LATE:
                     ref = w.at[MAT[i], some, pl.ds(0, cols // 2)]
+                elif i == KV:
+                    ref = w.at[pl.ds(K, 2), some]
                 else:
-                    ref = w.at[i, some]
+                    ref = w.at[MAT[i], some]
                 arrival(ref, wsend.at[0], wrecv.at[i])
 
     def t_send(owner, ch, s, d):
@@ -337,7 +342,8 @@
                 gain = tok[zz * NC + c, pl.ds(rows, GAIN_ROWS), :].astype(F32)[0:1]
                 v = tok[zz * NC + c, at, :].astype(F32)
                 total += v * v
-                xn[zz, at, c * cols : (c + 1) * cols] = (v * gain).astype(BF16)
+                lane0 = pl.multiple_of((zz * NC + c) * cols, cols)
+                xn[at, pl.ds(lane0, cols)] = (v * gain).astype(BF16)
             ss[at, :] = total
             return 0
 
@@ -345,7 +351,7 @@
 
     def absorb(m, zz):
         here = pl.ds(pl.multiple_of(zz * NC * cols, NC * cols), NC * cols)
-        acc[m] += jnp.dot(xn[zz], w[m, here, :], preferred_element_type=F32)
+        acc[m] += jnp.dot(xn[:, here], w[m, here, :], preferred_element_type=F32)
 
     def each_far(lo, hi, call):
         def one(zz, _):
@@ -366,11 +372,24 @@
 
         lax.fori_loop(0, 3, one, 0)
 
-    def absorb_near(m, hi):
+    def absorb_near(hi):
         for key in in_order:
-            if key[0] == m:
+            if key[0] not in LATE:
                 wait_w(key)
-        each_far(0, hi, functools.partial(absorb, m))
+        from_end = jnp.where(z < nz // 2, z, nz - 1 - z)
+        for uu in range(nz // 2):
+
+            @pl.when(from_end == uu)
+            def _(uu=uu):
+                deep = min(uu + hi + 1, nz) * NC * cols
+                start = jnp.where(z < nz // 2, 0, d_model - deep)
+                here = pl.ds(pl.multiple_of(start, NC * cols), deep)
+
+                def one(m, _):
+                    acc[m] = jnp.dot(xn[:, here], w[m, here, :], preferred_element_type=F32)
+                    return 0
+
+                lax.fori_loop(0, 3, one, 0)
 
     def late_block(s):
         each_far(s, s, widen)
@@ -414,19 +433,17 @@
         lax.fori_loop(0, groups, one, 0)
 
     t_all = max(when_in[k] for k in in_order if k[0] not in LATE)
-    t_w = {K: t_all - 1.8, Q: t_all - 0.7, V: t_all + 1.0}
+    t_near = t_all - 0.6
     t_tok = {0: 8.0}
     for e in events:
         if e[3] == "t":
             t_tok[e[4][0]] = max(t_tok.get(e[4][0], 0.0), e[0] + 2.0)
-    early = max([s for s in range(nz) if t_tok[s] < min(t_w.values())])
+    early = max([s for s in range(nz) if t_tok[s] < t_near - 0.5])
     steps = []
     for s in range(early + 1):
         call = functools.partial(each_far, s, s, widen)
-        steps.append((t_tok[s] + 5.0, 0.4, "widen_%d" % s, call))
-    for m in (K, V, Q):
-        call = functools.partial(absorb_near, m, early)
-        steps.append((t_w[m], 1.2, "absorb_m%d" % m, call))
+        steps.append((min(t_tok[s] + 5.0, t_near - 0.1), 0.4, "widen_%d" % s, call))
+    steps.append((t_near, 2.8, "absorb_near", functools.partial(absorb_near, early)))
     steps.sort(key=lambda e: e[0])
     for s in range(early + 1, nz):
         call = functools.partial(late_block, s)
@@ -462,6 +479,12 @@
     events.append((T0 + 4.5, 2, 0, "z", answer))
     events.sort(key=lambda e: e[:3])
     mark(None)
+    copies[3].start()
+    pgain_copy.start()
+    for g in range(cols // min(128, cols)):
+        half_l = min(128, cols)
+        qkv[V, g, :, half_l:] = jnp.ones((rows, half_l), BF16)
+    ss[...] = jnp.zeros_like(ss)
     now = T0
     while events or steps:
         if events and (events[0][0] <= now or not steps):
@@ -533,14 +556,15 @@
     def hop_in(t, ch, a):
         zz = real(t)
         way = near if a == 0 else 1 - near
-        i = (way * nz + zz) * RCH + ch
+        i = jnp.where((zz == z) & (way == 0), nz, zz) * RCH + ch
         arrival(rin.at[way, zz, chunk(ch)], rsend.at[0], rrecv.at[i])
         return rin[way, zz, chunk(ch), :].astype(F32)
 
     def hop_out(t, ch, a, value):
         zz = real(t)
         way = near if a == 0 else 1 - near
-        i = (way * nz + zz) * RCH + ch
+        hit = z + (sigma if a == 0 else -sigma)
+        i = jnp.where((zz == hit) & (way == 0), nz, zz) * RCH + ch
         sout[zz, chunk(ch), :] = value.astype(BF16)
         to = mp + NC * (sigma if a == 0 else -sigma)
         remote(
@@ -599,6 +623,7 @@
                 hop_out(t, ch, a, value)
 
     mark("squares")
+    pgain_copy.wait()
     half = 128
     for k in range(1, n_mp):
         other = {"mp": lax.rem(mp + k, n_mp)}
@@ -614,7 +639,7 @@
         piece_t = jnp.transpose(
             jnp.broadcast_to(post[:, r * half : (r + 1) * half], (128, half))
         )
-        scale_out[r * half : (r + 1) * half, :] = piece_t[:, 0:1] * pgain_in[...].astype(F32).reshape(1, cols)
+        scale_out[r * half : (r + 1) * half, :] = piece_t[:, 0:1] * pgain_v[...].astype(F32).reshape(1, cols)
 
     mark("drain")
     w_rows = int(sum(msg.size for msg in by_key.values())) * blk // 4
@@ -656,13 +681,15 @@
             jax.ShapeDtypeStruct((rows, cols), F32),
             jax.ShapeDtypeStruct((rows, cols), F32),
         ),
-        in_specs=[any_spec, vmem, any_spec, any_spec, any_spec, vmem],
+        in_specs=[any_spec] * 6,
         out_specs=(vmem, vmem),
         scratch_shapes=[
+            pltpu.VMEM((cols,), BF16),
+            pltpu.VMEM((cols,), BF16),
             pltpu.VMEM((n_mp, rows + GAIN_ROWS, cols), BF16),
             pltpu.VMEM((4, n_dp * blk, cols), BF16),
             pltpu.VMEM((heads, seq, seq), BF16),
-            pltpu.VMEM((nz, rows, NC * cols), BF16),
+            pltpu.VMEM((rows, n_mp * cols), BF16),
             pltpu.VMEM((rows, cols), F32),
             pltpu.VMEM((3, rows, cols), F32),
             pltpu.VMEM((3, cols // lanes, rows, 2 * lanes), BF16),
@@ -673,7 +700,7 @@
             pltpu.VMEM((2, nz, rows, cols), BF16),
             pltpu.VMEM((nz, rows, cols), BF16),
             pltpu.VMEM((n_mp, 8, rows), F32),
-            dma((4,)),
+            dma((6,)),
             pltpu.SemaphoreType.REGULAR,
             dma((1,)),
             dma((n_slots,)),
@@ -686,7 +713,7 @@
             dma((1,)),
             dma((2 * nz,)),
             dma((1,)),
-            dma((2 * nz * RCH,)),
+            dma(((nz + 1) * RCH,)),
             dma((1,)),
             dma((1,)),
         ],

time: 104 us -> 102 us (0.981)
  Pallas kernels: 101 us -> 99.3 us
    pallas_call x1, Pallas kernels: 101 us -> 99.3 us  [on_device(): pl.pallas_call(functools.partial(body, nz), out_shape=(jax.ShapeDtypeStru...]
where the time goes in v5:
time: 102 us
  Pallas kernels  99.3 us (97%)
  other arithmetic  2.09 us (2%)
    pallas_call x1, Pallas kernels, on_device(): pl.pallas_call(functools.partial(body, nz), out_shape=(jax.ShapeDtypeStru...  99.3 us
    convert_element_type x1, other arithmetic, on_device(): normed = (stream * scale).astype(BF16)  2.09 us

profile of v5, /device:TPU:1, one launch (start us, length us, event | category | flops | bytes accessed | tf_op | source)
XLA Modules:
  0.0 102.1 jit_solution(13628962773874440785)
XLA Ops:
  0.6 0.0 copy-start
  0.6 99.3 %shard_map.77 = (f32[512,256]{1,0:T(8,128)}, f32[512,256]{1,0:T(8,128)}) custom-call(bf16[512,256]{1,0:T(8,128)(2,1)} %tok_in.1, bf16[256]{0:T(256)(128)(2,1)} %gain_in.1, bf16[3,48,256]{2,1,0:T(8,128)(2,1)} %wi_in.1, bf16[48,256]{1,0:T(8,128)(2,1)} %bitcast.1, bf16[4,512,512]{2,1,0:T(8,128)(2,1)} %bias_in.1, bf16[256]{0:T(256)(128)(2,1)} %pgain_in.1), custom_call_target="tpu_custom_call" | custom-call | tf_op jit(solution)/shard_map/pallas_call | solution.py:678
  100.0 0.0 copy-done
  100.0 2.1 %multiply_convert_fusion = (bf16[512,256]{1,0:T(8,128)(2,1)}, bf16[512,256]{1,0:T(8,128)(2,1)}) fusion(f32[512,256]{1,0:T(8,128)} %get-tuple-element.5, f32[512,256]{1,0:T(8,128)} %get-tuple-element.4, bf16[512,256]{1,0:T(8,128)(2,1)S(1)} %copy-done), kind=kLoop, calls=%fused_computation | loop fusion | flops 786432 | bytes 1835008 | tf_op jit(solution)/shard_map/convert_element_type | solution.py:725
Async XLA Ops:
  0.6 99.3 %copy-start = (bf16[512,256]{1,0:T(8,128)(2,1)S(1)}, bf16[512,256]{1,0:T(8,128)(2,1)}, u32[]{:S(2)}) copy-start(bf16[512,256]{1,0:T(8,128)(2,1)} %tok_in.1) | copy-start | bytes 786436

commit v6 on v5

--- a/solution.py
+++ b/solution.py
@@ -25,7 +25,7 @@
 RCH = 4
 LATE_START = 0.0
 FIRST_LATE = 2.5
-LATE_RANK = 8.0
+LATE_RANK = 6.0
 
 
 class Msg:

time: 102 us -> 102 us (level)
  no operation moved by 1% of the time
where the time goes in v6:
time: 102 us
  Pallas kernels  99.2 us (97%)
  other arithmetic  2.09 us (2%)
    pallas_call x1, Pallas kernels, on_device(): pl.pallas_call(functools.partial(body, nz), out_shape=(jax.ShapeDtypeStru...  99.2 us
    convert_element_type x1, other arithmetic, on_device(): normed = (stream * scale).astype(BF16)  2.09 us

profile of v6, /device:TPU:1, one launch (start us, length us, event | category | flops | bytes accessed | tf_op | source)
XLA Modules:
  0.0 102.0 jit_solution(5979744215964243935)
XLA Ops:
  0.6 0.0 copy-start
  0.6 99.2 %shard_map.77 = (f32[512,256]{1,0:T(8,128)}, f32[512,256]{1,0:T(8,128)}) custom-call(bf16[512,256]{1,0:T(8,128)(2,1)} %tok_in.1, bf16[256]{0:T(256)(128)(2,1)} %gain_in.1, bf16[3,48,256]{2,1,0:T(8,128)(2,1)} %wi_in.1, bf16[48,256]{1,0:T(8,128)(2,1)} %bitcast.1, bf16[4,512,512]{2,1,0:T(8,128)(2,1)} %bias_in.1, bf16[256]{0:T(256)(128)(2,1)} %pgain_in.1), custom_call_target="tpu_custom_call" | custom-call | tf_op jit(solution)/shard_map/pallas_call | solution.py:678
  99.9 0.0 copy-done
  99.9 2.1 %multiply_convert_fusion = (bf16[512,256]{1,0:T(8,128)(2,1)}, bf16[512,256]{1,0:T(8,128)(2,1)}) fusion(f32[512,256]{1,0:T(8,128)} %get-tuple-element.5, f32[512,256]{1,0:T(8,128)} %get-tuple-element.4, bf16[512,256]{1,0:T(8,128)(2,1)S(1)} %copy-done), kind=kLoop, calls=%fused_computation | loop fusion | flops 786432 | bytes 1835008 | tf_op jit(solution)/shard_map/convert_element_type | solution.py:725
Async XLA Ops:
  0.6 99.2 %copy-start = (bf16[512,256]{1,0:T(8,128)(2,1)S(1)}, bf16[512,256]{1,0:T(8,128)(2,1)}, u32[]{:S(2)}) copy-start(bf16[512,256]{1,0:T(8,128)(2,1)} %tok_in.1) | copy-start | bytes 786436
